TPU v7x, 32 devices: a whole 2x2x4 slice. The times are simulated.
32 devices in a mesh: section: 4 (over z), expert: 8 (over y, x, core).
Axes of the slice: x: 2, y: 2, z: 4, core: 2. Of those that a mesh axis runs over, the one named last changes fastest.
Arguments:
- act_a: bfloat16 [4, 512, 3584], P('section', 'expert'), may hold values from -6 to 6
- act_b: bfloat16 [4, 512, 3584], P('section', 'expert'), may hold values from -6 to 6
- grad_b: bfloat16 [4, 512, 3584], P('section', 'expert'), may hold values from -6 to 6
- ids_a: int32 [4, 512, 2], P('section', 'expert'), may hold values from 0 to 3, all different within a row; in each aligned block of 64 rows (0 to 63, 64 to 127, ..., all dimensions but the last counted through in order) at most 48 rows name the same one
- ids_b: int32 [4, 512, 2], P('section', 'expert'), may hold values from 0 to 3, all different within a row; in each aligned block of 64 rows (0 to 63, 64 to 127, ..., all dimensions but the last counted through in order) at most 48 rows name the same one
- scores_a: float32 [4, 512, 2], P('section', 'expert'), may hold values from 0.1 to 1
- scores_b: float32 [4, 512, 2], P('section', 'expert'), may hold values from 0.1 to 1
- w_gate: bfloat16 [4, 8, 3584, 512], P('section', 'expert'), may hold values from -0.09375 to 0.09375
- w_up: bfloat16 [4, 8, 3584, 512], P('section', 'expert'), may hold values from -0.09375 to 0.09375
- w_down: bfloat16 [4, 8, 512, 3584], P('section', 'expert'), may hold values from -0.1875 to 0.1875
Outputs:
- out_a: bfloat16 [4, 512, 3584], P('section', 'expert')
- grad_in_b: bfloat16 [4, 512, 3584], P('section', 'expert')
Inputs may be any that keep to these rules, and one draw needn't show every extreme that they name: `ids_a`: each row names 2 different experts. Within the 64 rows of one device no expert is named by more than 48 rows, and in some device's rows some expert is named by exactly 48. `ids_b`: as for ids_a.
All inputs are finite; a program needn't handle non-finite values.
Results may differ from a plain program's by a relative error of at most 0.0072.
Values may be sent and summed in bfloat16 or wider, within the bound.
No kernel may reach another device: no remote copies, remote signals or barrier semaphores. Data moves between devices by JAX's collectives and lax.ppermute only.
A program may use at most 128 MiB of HBM per device.

v0:
```python
import jax
import jax.numpy as jnp
from jax import lax
from jax.sharding import PartitionSpec as P


def shift(block, axis, distance):
    count = lax.axis_size(axis)
    return lax.ppermute(block, axis, [((i - distance) % count, i) for i in range(count)])


def chip_bits(count):
    return (count // 2).bit_length() - 1


def step_bit(core, step, count):
    bits = chip_bits(count)
    return step if core == 0 else bits - 1 - step


def exchange(block, step):
    count = lax.axis_size("expert")
    route = []
    for i in range(count):
        bit = step_bit(i % 2, step, count)
        route.append((i, i ^ (2 << bit)))
    return lax.ppermute(block, "expert", route)


def swap_cores(block):
    count = lax.axis_size("expert")
    return lax.ppermute(block, "expert", [(i, i ^ 1) for i in range(count)])


def gather(block, dim):
    for step in range(chip_bits(lax.axis_size("expert")) - 1):
        other = exchange(block, step)
        block = jnp.concatenate([block, other], dim)
    return block


def last_exchange(block):
    return exchange(block, chip_bits(lax.axis_size("expert")) - 1)


def spread_back(block):
    for step in reversed(range(chip_bits(lax.axis_size("expert")) - 1)):
        half = block.shape[0] // 2
        other = exchange(block[half:], step)
        block = (block[:half].astype(jnp.float32) + other.astype(jnp.float32)).astype(jnp.bfloat16)
    return block


def slots(ids, wanted, tok_rows, capacity):
    chosen = jnp.any(ids == wanted, 0, keepdims=True)
    total = ids.shape[1]
    at = jnp.arange(total, dtype=jnp.int32)
    earlier = (at[:, None] < at[None, :]) & (at[:, None] // tok_rows == at[None, :] // tok_rows)
    before = jnp.dot(
        chosen.astype(jnp.bfloat16), earlier.astype(jnp.bfloat16), preferred_element_type=jnp.float32
    ).astype(jnp.int32)
    return jnp.where(chosen, (at // tok_rows)[None, :] * capacity + before, -1)


def expert_weight(ids, weights, wanted):
    return jnp.sum(jnp.where(ids == wanted, weights, 0.0), 0, keepdims=True)


def pick(slot_of, rows_out):
    return slot_of == jnp.arange(rows_out, dtype=jnp.int32)[:, None]


def matmul(left, right):
    return jnp.dot(left, right, preferred_element_type=jnp.float32)


def contract_last(left, right):
    return lax.dot_general(left, right, (((1,), (1,)), ((), ())), preferred_element_type=jnp.float32)


def contract_first(left, right):
    return lax.dot_general(left, right, (((0,), (0,)), ((), ())), preferred_element_type=jnp.float32)


PARTS = {"x": 1, "g": 2, "a": 2, "rb": 2, "ra": 2}


def pieces(block, count):
    size = block.shape[-1] // count
    return [block[..., c * size : (c + 1) * size] for c in range(count)]


def shards(act_a, act_b, grad_b, ids_a, ids_b, scores_a, scores_b, w_gate, w_up, w_down):
    count = lax.axis_size("expert")
    experts = count // 2
    tok_rows = act_a.shape[1]
    top_count = ids_a.shape[2]
    capacity = 3 * tok_rows * top_count // (2 * experts)
    gate_w, up_w, down_w = w_gate[0, 0], w_up[0, 0], w_down[0, 0]

    me = lax.axis_index("expert")
    core = me % 2
    chip = me // 2
    last = chip_bits(count) - 1
    other_chip = jnp.where(core == 0, chip ^ (1 << step_bit(0, last, count)), chip ^ (1 << step_bit(1, last, count)))

    width = act_a.shape[2]

    upstream = []
    for x in pieces(grad_b, PARTS["g"]):
        upstream.append(shift(x, "section", -1)[0])
    raw_b = [gather(x, 0) for x in pieces(act_b[0], PARTS["x"])]
    incoming = []
    for x in pieces(act_a, PARTS["a"]):
        incoming.append(shift(x, "section", 1)[0])

    meta = gather(
        jnp.concatenate(
            [ids_a[0].T.astype(jnp.float32), ids_b[0].T.astype(jnp.float32), scores_a[0].T, scores_b[0].T], 0
        ),
        1,
    )
    k = top_count
    all_a, all_b = meta[:k].astype(jnp.int32), meta[k : 2 * k].astype(jnp.int32)
    weights_a = meta[2 * k : 3 * k] / jnp.sum(meta[2 * k : 3 * k], 0, keepdims=True)
    weights_b = meta[3 * k :] / jnp.sum(meta[3 * k :], 0, keepdims=True)
    held = all_a.shape[1] // tok_rows * capacity

    def places(ids):
        keep = pick(slots(ids, chip, tok_rows, capacity), held)
        give = pick(slots(ids, other_chip, tok_rows, capacity), held)
        return keep, give

    keep_a, give_a = places(all_a)
    keep_b, give_b = places(all_b)
    onehot_a = jnp.concatenate([keep_a, give_a], 0).astype(jnp.bfloat16)
    onehot_b = jnp.concatenate([keep_b, give_b], 0).astype(jnp.bfloat16)
    spread_a = jnp.concatenate(
        [
            jnp.where(keep_a, expert_weight(all_a, weights_a, chip), 0.0),
            jnp.where(give_a, expert_weight(all_a, weights_a, other_chip), 0.0),
        ],
        0,
    ).astype(jnp.bfloat16)
    scale_b = jnp.concatenate(
        [
            jnp.sum(jnp.where(keep_b, expert_weight(all_b, weights_b, chip), 0.0), 1, keepdims=True),
            jnp.sum(jnp.where(give_b, expert_weight(all_b, weights_b, other_chip), 0.0), 1, keepdims=True),
        ],
        0,
    )

    def deliver(raw, onehot, scale=None):
        out = []
        for x in raw:
            picked = matmul(onehot, x)
            picked = (picked if scale is None else picked * scale).astype(jnp.bfloat16)
            mine, theirs = picked[:held], picked[held:]
            got = last_exchange(theirs)
            mine_there = swap_cores(mine)
            got_there = swap_cores(got)
            out.append(jnp.concatenate([mine, got, mine_there, got_there], 0))
        return out

    rows_x = deliver(raw_b, onehot_b)
    rows_g = deliver([gather(x, 0) for x in upstream], onehot_b, scale_b)
    rows_a = deliver([gather(x, 0) for x in incoming], onehot_a)

    def give_back(parts, spread):
        out = []
        for part in parts:
            other = swap_cores(part[2 * held :])
            summed = (part[: 2 * held].astype(jnp.float32) + other.astype(jnp.float32)).astype(jnp.bfloat16)
            back = last_exchange(summed[held:])
            tokens = contract_first(spread, jnp.concatenate([summed[:held], back], 0)).astype(jnp.bfloat16)
            out.append(spread_back(tokens))
        return jnp.concatenate(out, 1)

    def up(rows, weight):
        total, size = 0.0, width // len(rows)
        for c, x in enumerate(rows):
            total = matmul(x, weight[c * size : (c + 1) * size]) + total
        return total

    first_b, second_b = lax.optimization_barrier((up(rows_x, gate_w), up(rows_x, up_w)))
    dact, size = 0.0, width // len(rows_g)
    for c, x in enumerate(rows_g):
        dact = contract_last(x, down_w[:, c * size : (c + 1) * size]) + dact
    dact = lax.optimization_barrier(dact)
    sig = jax.nn.sigmoid(first_b)
    dfirst = (dact * second_b * sig * (1.0 + first_b * (1.0 - sig))).astype(jnp.bfloat16)
    dsecond = (dact * first_b * sig).astype(jnp.bfloat16)
    dfirst, dsecond = lax.optimization_barrier((dfirst, dsecond))
    parts_b, size = [], width // PARTS["rb"]
    for c in range(PARTS["rb"]):
        part = contract_last(dfirst, gate_w[c * size : (c + 1) * size])
        parts_b.append((part + contract_last(dsecond, up_w[c * size : (c + 1) * size])).astype(jnp.bfloat16))
    grad_in_b = give_back(parts_b, onehot_b)

    first_a, second_a = lax.optimization_barrier((up(rows_a, gate_w), up(rows_a, up_w)))
    hidden = lax.optimization_barrier((jax.nn.silu(first_a) * second_a).astype(jnp.bfloat16))
    parts_a, size = [], width // PARTS["ra"]
    for c in range(PARTS["ra"]):
        parts_a.append(matmul(hidden, down_w[:, c * size : (c + 1) * size]).astype(jnp.bfloat16))
    out_a = give_back(parts_a, spread_a)
    return (out_a[None], grad_in_b[None])


def solution(mesh):
    tokens = P("section", "expert", None)
    weights = P("section", "expert", None, None)
    return jax.shard_map(
        shards,
        mesh=mesh,
        in_specs=(tokens,) * 7 + (weights,) * 3,
        out_specs=(tokens, tokens),
        check_vma=False,
    )
```

profile of v0, /device:TPU:0, one launch (start us, length us, event | category | flops | bytes accessed | tf_op | source)
XLA Modules:
  0.0 115.9 jit_solution(16907178924029464191)
XLA Ops:
  0.6 0.7 convert_bitcast_fusion
  1.3 0.7 pad_maximum_fusion.12
  2.0 3.0 %collective-permute-start = (f32[8,64]{1,0:T(8,128)S(1)}, f32[8,64]{1,0:T(8,128)S(1)}, u32[]{:S(2)}, u32[]{:S(2)}) collective-permute-start(f32[8,64]{1,0:T(8,128)S(1)} %pad_maximum_fusion.12), channel_id=1, source_target_pairs={{0,2},{1,5},{2,0},{3,7},{4,6},{5,1},{6,4},{7,3},{8,10},{9,13},{10,... | collective-permute-start | bytes 6152 | tf_op jit(solution)/shard_map/ppermute | solution.py:27
  5.1 1.1 fusion.141
  6.2 4.1 %collective-permute-start.22 = (bf16[1,64,1792]{2,1,0:T(8,128)(2,1)S(1)}, bf16[1,64,1792]{2,1,0:T(8,128)(2,1)S(1)}, u32[]{:S(2)}, u32[]{:S(2)}) collective-permute-start(bf16[1,64,1792]{2,1,0:T(8,128)(2,1)S(1)} %get-tuple-element.44), channel_id=1, source_target_pairs={{8,0},{16,8},{24,16},{0,24},{9,1},{17,9},{25,17},{1,25},{10,2},{18... | collective-permute-start | bytes 688136 | tf_op jit(solution)/shard_map/ppermute | solution.py:9
  10.3 0.4 collective-permute-start.17
  10.8 1.1 fusion.142
  11.9 1.6 %collective-permute-start.6 = (bf16[1,64,1792]{2,1,0:T(8,128)(2,1)S(1)}, bf16[1,64,1792]{2,1,0:T(8,128)(2,1)S(1)}, u32[]{:S(2)}, u32[]{:S(2)}) collective-permute-start(bf16[1,64,1792]{2,1,0:T(8,128)(2,1)S(1)} %get-tuple-element.46), channel_id=1, source_target_pairs={{24,0},{0,8},{8,16},{16,24},{25,1},{1,9},{9,17},{17,25},{26,2},{2,... | collective-permute-start | bytes 688136 | tf_op jit(solution)/shard_map/ppermute | solution.py:9
  13.6 0.8 pad_maximum_fusion.13
  15.7 0.7 collective-permute-done.22
  16.4 1.5 %collective-permute-start.23 = (bf16[64,1792]{1,0:T(8,128)(2,1)S(1)}, bf16[64,1792]{1,0:T(8,128)(2,1)S(1)}, u32[]{:S(2)}, u32[]{:S(2)}) collective-permute-start(bf16[64,1792]{1,0:T(8,128)(2,1)S(1)} %bitcast.127), channel_id=1, source_target_pairs={{0,2},{1,5},{2,0},{3,7},{4,6},{5,1},{6,4},{7,3},{8,10},{9,13},{10,... | collective-permute-start | bytes 688136 | tf_op jit(solution)/shard_map/ppermute | solution.py:27
  17.9 3.4 %collective-permute-done.17 = bf16[1,64,1792]{2,1,0:T(8,128)(2,1)S(1)} collective-permute-done((bf16[1,64,1792]{2,1,0:T(8,128)(2,1)S(1)}, bf16[1,64,1792]{2,1,0:T(8,128)(2,1)S(1)}, u32[]{:S(2)}, u32[]{:S(2)}) %collective-permute-start.17) | collective-permute-done | bytes 229408 | tf_op jit(solution)/shard_map/ppermute | solution.py:9
  21.3 1.5 %collective-permute-start.18 = (bf16[64,1792]{1,0:T(8,128)(2,1)S(1)}, bf16[64,1792]{1,0:T(8,128)(2,1)S(1)}, u32[]{:S(2)}, u32[]{:S(2)}) collective-permute-start(bf16[64,1792]{1,0:T(8,128)(2,1)S(1)} %bitcast.125), channel_id=1, source_target_pairs={{0,2},{1,5},{2,0},{3,7},{4,6},{5,1},{6,4},{7,3},{8,10},{9,13},{10,... | collective-permute-start | bytes 688136 | tf_op jit(solution)/shard_map/ppermute | solution.py:27
  22.8 4.2 %collective-permute-done.6 = bf16[1,64,1792]{2,1,0:T(8,128)(2,1)S(1)} collective-permute-done((bf16[1,64,1792]{2,1,0:T(8,128)(2,1)S(1)}, bf16[1,64,1792]{2,1,0:T(8,128)(2,1)S(1)}, u32[]{:S(2)}, u32[]{:S(2)}) %collective-permute-start.6) | collective-permute-done | bytes 229408 | tf_op jit(solution)/shard_map/ppermute | solution.py:9
  27.1 1.5 %collective-permute-start.7 = (bf16[64,1792]{1,0:T(8,128)(2,1)S(1)}, bf16[64,1792]{1,0:T(8,128)(2,1)S(1)}, u32[]{:S(2)}, u32[]{:S(2)}) collective-permute-start(bf16[64,1792]{1,0:T(8,128)(2,1)S(1)} %bitcast.109), channel_id=1, source_target_pairs={{0,2},{1,5},{2,0},{3,7},{4,6},{5,1},{6,4},{7,3},{8,10},{9,13},{10,... | collective-permute-start | bytes 688136 | tf_op jit(solution)/shard_map/ppermute | solution.py:27
  28.6 1.7 %collective-permute-done.1 = bf16[1,64,1792]{2,1,0:T(8,128)(2,1)S(1)} collective-permute-done((bf16[1,64,1792]{2,1,0:T(8,128)(2,1)S(1)}, bf16[1,64,1792]{2,1,0:T(8,128)(2,1)S(1)}, u32[]{:S(2)}, u32[]{:S(2)}) %collective-permute-start.1) | collective-permute-done | bytes 229408 | tf_op jit(solution)/shard_map/ppermute | solution.py:9
  30.3 1.5 %collective-permute-start.2 = (bf16[64,1792]{1,0:T(8,128)(2,1)S(1)}, bf16[64,1792]{1,0:T(8,128)(2,1)S(1)}, u32[]{:S(2)}, u32[]{:S(2)}) collective-permute-start(bf16[64,1792]{1,0:T(8,128)(2,1)S(1)} %bitcast.111), channel_id=1, source_target_pairs={{0,2},{1,5},{2,0},{3,7},{4,6},{5,1},{6,4},{7,3},{8,10},{9,13},{10,... | collective-permute-start | bytes 688136 | tf_op jit(solution)/shard_map/ppermute | solution.py:27
  31.8 1.5 %convolution_convert_fusion = bf16[192,3584]{1,0:T(8,128)(2,1)S(1)} fusion(bf16[64,3584]{1,0:T(8,128)(2,1)S(1)} %collective-permute-done.27, bf16[64,3584]{1,0:T(8,128)(2,1)} %bitcast.108, pred[96,128]{1,0:T(32,128)(4,1)S(1)} %iota_compare_fusion.1, pred[96,128]{1,0:T(32,128)(4,1)S(1)} %iota_compare_fusion.2), kind=kOutput, calls=%fused_computation | convolution fusion | flops 178708480 | bytes 2318336 | tf_op jit(solution)/shard_map/dot_general | solution.py:74
  33.4 1.6 %collective-permute-start.28 = (bf16[96,3584]{1,0:T(8,128)(2,1)S(1)}, bf16[96,3584]{1,0:T(8,128)(2,1)S(1)}, u32[]{:S(2)}, u32[]{:S(2)}) collective-permute-start(bf16[96,3584]{1,0:T(8,128)(2,1)S(1)} %get-tuple-element.26), channel_id=1, source_target_pairs={{0,4},{1,3},{2,6},{3,1},{4,0},{5,7},{6,2},{7,5},{8,12},{9,11},{10,... | collective-permute-start | bytes 2064392 | tf_op jit(solution)/shard_map/ppermute | solution.py:27
  35.8 0.6 collective-permute-start.8
  36.4 2.0 %collective-permute-done.2 = bf16[64,1792]{1,0:T(8,128)(2,1)S(1)} collective-permute-done((bf16[64,1792]{1,0:T(8,128)(2,1)S(1)}, bf16[64,1792]{1,0:T(8,128)(2,1)S(1)}, u32[]{:S(2)}, u32[]{:S(2)}) %collective-permute-start.2) | collective-permute-done | bytes 229408 | tf_op jit(solution)/shard_map/ppermute | solution.py:27
  38.8 2.0 %collective-permute-start.3 = (bf16[96,1792]{1,0:T(8,128)(2,1)S(1)}, bf16[96,1792]{1,0:T(8,128)(2,1)S(1)}, u32[]{:S(2)}, u32[]{:S(2)}) collective-permute-start(bf16[96,1792]{1,0:T(8,128)(2,1)S(1)} %get-tuple-element.40), channel_id=1, source_target_pairs={{0,4},{1,3},{2,6},{3,1},{4,0},{5,7},{6,2},{7,5},{8,12},{9,11},{10,... | collective-permute-start | bytes 1032200 | tf_op jit(solution)/shard_map/ppermute | solution.py:27
  41.1 7.0 %collective-permute-done.8 = bf16[96,1792]{1,0:T(8,128)(2,1)S(1)} collective-permute-done((bf16[96,1792]{1,0:T(8,128)(2,1)S(1)}, bf16[96,1792]{1,0:T(8,128)(2,1)S(1)}, u32[]{:S(2)}, u32[]{:S(2)}) %collective-permute-start.8) | collective-permute-done | bytes 344096 | tf_op jit(solution)/shard_map/ppermute | solution.py:27
  48.2 1.6 %collective-permute-start.24 = (bf16[96,1792]{1,0:T(8,128)(2,1)S(1)}, bf16[96,1792]{1,0:T(8,128)(2,1)S(1)}, u32[]{:S(2)}, u32[]{:S(2)}) collective-permute-start(bf16[96,1792]{1,0:T(8,128)(2,1)S(1)} %get-tuple-element.34), channel_id=1, source_target_pairs={{0,4},{1,3},{2,6},{3,1},{4,0},{5,7},{6,2},{7,5},{8,12},{9,11},{10,... | collective-permute-start | bytes 1032200 | tf_op jit(solution)/shard_map/ppermute | solution.py:27
  49.7 2.0 %collective-permute-done.3 = bf16[96,1792]{1,0:T(8,128)(2,1)S(1)} collective-permute-done((bf16[96,1792]{1,0:T(8,128)(2,1)S(1)}, bf16[96,1792]{1,0:T(8,128)(2,1)S(1)}, u32[]{:S(2)}, u32[]{:S(2)}) %collective-permute-start.3) | collective-permute-done | bytes 344096 | tf_op jit(solution)/shard_map/ppermute | solution.py:27
  51.8 0.5 collective-permute-start.5
  52.3 0.9 fusion.9
  53.2 2.3 %collective-permute-done.24 = bf16[96,1792]{1,0:T(8,128)(2,1)S(1)} collective-permute-done((bf16[96,1792]{1,0:T(8,128)(2,1)S(1)}, bf16[96,1792]{1,0:T(8,128)(2,1)S(1)}, u32[]{:S(2)}, u32[]{:S(2)}) %collective-permute-start.24) | collective-permute-done | bytes 344096 | tf_op jit(solution)/shard_map/ppermute | solution.py:27
  55.5 1.6 %collective-permute-start.19 = (bf16[96,1792]{1,0:T(8,128)(2,1)S(1)}, bf16[96,1792]{1,0:T(8,128)(2,1)S(1)}, u32[]{:S(2)}, u32[]{:S(2)}) collective-permute-start(bf16[96,1792]{1,0:T(8,128)(2,1)S(1)} %get-tuple-element.32), channel_id=1, source_target_pairs={{0,4},{1,3},{2,6},{3,1},{4,0},{5,7},{6,2},{7,5},{8,12},{9,11},{10,... | collective-permute-start | bytes 1032200 | tf_op jit(solution)/shard_map/ppermute | solution.py:27
  57.1 0.9 fusion.53
  58.0 0.9 fusion.16
  58.8 0.9 fusion.50
  59.7 0.6 collective-permute-start.20
  60.3 2.5 %collective-permute-done.19 = bf16[96,1792]{1,0:T(8,128)(2,1)S(1)} collective-permute-done((bf16[96,1792]{1,0:T(8,128)(2,1)S(1)}, bf16[96,1792]{1,0:T(8,128)(2,1)S(1)}, u32[]{:S(2)}, u32[]{:S(2)}) %collective-permute-start.19) | collective-permute-done | bytes 344096 | tf_op jit(solution)/shard_map/ppermute | solution.py:27
  62.8 0.5 collective-permute-start.30
  63.3 0.9 fusion.25
  64.5 0.9 fusion.56
  65.6 0.9 convolution_convert_fusion.2
  66.7 0.9 convolution_convert_fusion.1
  67.7 0.4 collective-permute-start.14
  68.1 1.6 %fusion = f32[384,512]{1,0:T(8,128)S(1)} fusion(bf16[1,1,3584,512]{3,2,1,0:T(8,128)(2,1)S(1)} %copy-done.1, bf16[96,3584]{1,0:T(8,128)(2,1)S(1)} %collective-permute-done.30, bf16[96,3584]{1,0:T(8,128)(2,1)S(1)} %collective-permute-done.29, bf16[96,3584]{1,0:T(8,128)(2,1)S(1)} %collective-permute-done.28, bf16[96,3584]{1,0:T(8,128)(2,1)S(1)} %get-tuple-element.25), kind=kOutput, calls=%fused_computation.1 | convolution fusion | flops 1420296192 | bytes 7208960 | tf_op jit(solution)/shard_map/dot_general | solution.py:74
  69.7 1.6 %fusion.2 = f32[384,512]{1,0:T(8,128)S(1)} fusion(bf16[1,1,3584,512]{3,2,1,0:T(8,128)(2,1)S(1)} %copy-done, bf16[96,3584]{1,0:T(8,128)(2,1)S(1)} %collective-permute-done.30, bf16[96,3584]{1,0:T(8,128)(2,1)S(1)} %collective-permute-done.29, bf16[96,3584]{1,0:T(8,128)(2,1)S(1)} %collective-permute-done.28, bf16[96,3584]{1,0:T(8,128)(2,1)S(1)} %get-tuple-element.25), kind=kOutput, calls=%fused_computation.3 | convolution fusion | flops 1420296192 | bytes 7208960 | tf_op jit(solution)/shard_map/dot_general | solution.py:74
  71.3 0.5 multiply_convert_fusion
  71.9 0.9 fusion.14
  72.8 0.9 fusion.4
  74.2 1.6 %collective-permute-start.12 = (bf16[96,1792]{1,0:T(8,128)(2,1)S(1)}, bf16[96,1792]{1,0:T(8,128)(2,1)S(1)}, u32[]{:S(2)}, u32[]{:S(2)}) collective-permute-start(bf16[96,1792]{1,0:T(8,128)(2,1)S(1)} %get-tuple-element.36), channel_id=1, source_target_pairs={{0,4},{1,3},{2,6},{3,1},{4,0},{5,7},{6,2},{7,5},{8,12},{9,11},{10,... | collective-permute-start | bytes 1032200 | tf_op jit(solution)/shard_map/ppermute | solution.py:27
  75.7 0.3 add_convert_fusion.2
  76.1 0.6 collective-permute-start.15
  76.7 0.9 fusion.18
  77.6 3.8 %collective-permute-done.12 = bf16[96,1792]{1,0:T(8,128)(2,1)S(1)} collective-permute-done((bf16[96,1792]{1,0:T(8,128)(2,1)S(1)}, bf16[96,1792]{1,0:T(8,128)(2,1)S(1)}, u32[]{:S(2)}, u32[]{:S(2)}) %collective-permute-start.12) | collective-permute-done | bytes 344096 | tf_op jit(solution)/shard_map/ppermute | solution.py:27
  81.8 0.9 collective-permute-start.13
  82.7 0.9 fusion.5
  83.8 2.5 %collective-permute-done.15 = bf16[96,1792]{1,0:T(8,128)(2,1)S(1)} collective-permute-done((bf16[96,1792]{1,0:T(8,128)(2,1)S(1)}, bf16[96,1792]{1,0:T(8,128)(2,1)S(1)}, u32[]{:S(2)}, u32[]{:S(2)}) %collective-permute-start.15) | collective-permute-done | bytes 344096 | tf_op jit(solution)/shard_map/ppermute | solution.py:27
  86.7 0.9 collective-permute-start.16
  88.0 4.8 %collective-permute-done.16 = bf16[64,1792]{1,0:T(8,128)(2,1)S(1)} collective-permute-done((bf16[64,1792]{1,0:T(8,128)(2,1)S(1)}, bf16[64,1792]{1,0:T(8,128)(2,1)S(1)}, u32[]{:S(2)}, u32[]{:S(2)}) %collective-permute-start.16) | collective-permute-done | bytes 229408 | tf_op jit(solution)/shard_map/ppermute | solution.py:27
  93.0 1.6 %collective-permute-start.32 = (bf16[96,1792]{1,0:T(8,128)(2,1)S(1)}, bf16[96,1792]{1,0:T(8,128)(2,1)S(1)}, u32[]{:S(2)}, u32[]{:S(2)}) collective-permute-start(bf16[96,1792]{1,0:T(8,128)(2,1)S(1)} %get-tuple-element.28), channel_id=1, source_target_pairs={{0,4},{1,3},{2,6},{3,1},{4,0},{5,7},{6,2},{7,5},{8,12},{9,11},{10,... | collective-permute-start | bytes 1032200 | tf_op jit(solution)/shard_map/ppermute | solution.py:27
  94.9 0.6 collective-permute-start.35
  95.4 5.8 %collective-permute-done.32 = bf16[96,1792]{1,0:T(8,128)(2,1)S(1)} collective-permute-done((bf16[96,1792]{1,0:T(8,128)(2,1)S(1)}, bf16[96,1792]{1,0:T(8,128)(2,1)S(1)}, u32[]{:S(2)}, u32[]{:S(2)}) %collective-permute-start.32) | collective-permute-done | bytes 344096 | tf_op jit(solution)/shard_map/ppermute | solution.py:27
  101.6 0.7 collective-permute-start.33
  102.3 0.8 maximum_bitcast_fusion
  103.1 5.5 %collective-permute-done.35 = bf16[96,1792]{1,0:T(8,128)(2,1)S(1)} collective-permute-done((bf16[96,1792]{1,0:T(8,128)(2,1)S(1)}, bf16[96,1792]{1,0:T(8,128)(2,1)S(1)}, u32[]{:S(2)}, u32[]{:S(2)}) %collective-permute-start.35) | collective-permute-done | bytes 344096 | tf_op jit(solution)/shard_map/ppermute | solution.py:27
  109.0 0.7 collective-permute-start.36
  109.8 5.3 %collective-permute-done.36 = bf16[64,1792]{1,0:T(8,128)(2,1)S(1)} collective-permute-done((bf16[64,1792]{1,0:T(8,128)(2,1)S(1)}, bf16[64,1792]{1,0:T(8,128)(2,1)S(1)}, u32[]{:S(2)}, u32[]{:S(2)}) %collective-permute-start.36) | collective-permute-done | bytes 229408 | tf_op jit(solution)/shard_map/ppermute | solution.py:27
  115.1 0.8 maximum_bitcast_fusion.1
  (91 shorter events, 6.8 us)
Async XLA Ops:
  2.0 11.5 %collective-permute-start = (f32[8,64]{1,0:T(8,128)S(1)}, f32[8,64]{1,0:T(8,128)S(1)}, u32[]{:S(2)}, u32[]{:S(2)}) collective-permute-start(f32[8,64]{1,0:T(8,128)S(1)} %pad_maximum_fusion.12), channel_id=1, source_target_pairs={{0,2},{1,5},{2,0},{3,7},{4,6},{5,1},{6,4},{7,3},{8,10},{9,13},{10,... | collective-permute-start | bytes 6152 | tf_op jit(solution)/shard_map/ppermute | solution.py:27
  5.1 26.7 %collective-permute-start.27 = (bf16[64,3584]{1,0:T(8,128)(2,1)}, bf16[64,3584]{1,0:T(8,128)(2,1)S(1)}, u32[]{:S(2)}, u32[]{:S(2)}) collective-permute-start(bf16[64,3584]{1,0:T(8,128)(2,1)} %bitcast.107), channel_id=1, source_target_pairs={{0,2},{1,5},{2,0},{3,7},{4,6},{5,1},{6,4},{7,3},{8,10},{9,13},{10,... | collective-permute-start | bytes 1376264 | tf_op jit(solution)/shard_map/ppermute | solution.py:27
  6.2 10.2 %collective-permute-start.22 = (bf16[1,64,1792]{2,1,0:T(8,128)(2,1)S(1)}, bf16[1,64,1792]{2,1,0:T(8,128)(2,1)S(1)}, u32[]{:S(2)}, u32[]{:S(2)}) collective-permute-start(bf16[1,64,1792]{2,1,0:T(8,128)(2,1)S(1)} %get-tuple-element.44), channel_id=1, source_target_pairs={{8,0},{16,8},{24,16},{0,24},{9,1},{17,9},{25,17},{1,25},{10,2},{18... | collective-permute-start | bytes 688136 | tf_op jit(solution)/shard_map/ppermute | solution.py:9
  10.3 11.0 %collective-permute-start.17 = (bf16[1,64,1792]{2,1,0:T(8,128)(2,1)S(1)}, bf16[1,64,1792]{2,1,0:T(8,128)(2,1)S(1)}, u32[]{:S(2)}, u32[]{:S(2)}) collective-permute-start(bf16[1,64,1792]{2,1,0:T(8,128)(2,1)S(1)} %get-tuple-element.43), channel_id=1, source_target_pairs={{8,0},{16,8},{24,16},{0,24},{9,1},{17,9},{25,17},{1,25},{10,2},{18... | collective-permute-start | bytes 688136 | tf_op jit(solution)/shard_map/ppermute | solution.py:9
  11.9 15.2 %collective-permute-start.6 = (bf16[1,64,1792]{2,1,0:T(8,128)(2,1)S(1)}, bf16[1,64,1792]{2,1,0:T(8,128)(2,1)S(1)}, u32[]{:S(2)}, u32[]{:S(2)}) collective-permute-start(bf16[1,64,1792]{2,1,0:T(8,128)(2,1)S(1)} %get-tuple-element.46), channel_id=1, source_target_pairs={{24,0},{0,8},{8,16},{16,24},{25,1},{1,9},{9,17},{17,25},{26,2},{2,... | collective-permute-start | bytes 688136 | tf_op jit(solution)/shard_map/ppermute | solution.py:9
  13.5 16.8 %collective-permute-start.1 = (bf16[1,64,1792]{2,1,0:T(8,128)(2,1)S(1)}, bf16[1,64,1792]{2,1,0:T(8,128)(2,1)S(1)}, u32[]{:S(2)}, u32[]{:S(2)}) collective-permute-start(bf16[1,64,1792]{2,1,0:T(8,128)(2,1)S(1)} %get-tuple-element.45), channel_id=1, source_target_pairs={{24,0},{0,8},{8,16},{16,24},{25,1},{1,9},{9,17},{17,25},{26,2},{2,... | collective-permute-start | bytes 688136 | tf_op jit(solution)/shard_map/ppermute | solution.py:9
  16.4 18.6 %collective-permute-start.23 = (bf16[64,1792]{1,0:T(8,128)(2,1)S(1)}, bf16[64,1792]{1,0:T(8,128)(2,1)S(1)}, u32[]{:S(2)}, u32[]{:S(2)}) collective-permute-start(bf16[64,1792]{1,0:T(8,128)(2,1)S(1)} %bitcast.127), channel_id=1, source_target_pairs={{0,2},{1,5},{2,0},{3,7},{4,6},{5,1},{6,4},{7,3},{8,10},{9,13},{10,... | collective-permute-start | bytes 688136 | tf_op jit(solution)/shard_map/ppermute | solution.py:27
  21.3 17.4 %collective-permute-start.18 = (bf16[64,1792]{1,0:T(8,128)(2,1)S(1)}, bf16[64,1792]{1,0:T(8,128)(2,1)S(1)}, u32[]{:S(2)}, u32[]{:S(2)}) collective-permute-start(bf16[64,1792]{1,0:T(8,128)(2,1)S(1)} %bitcast.125), channel_id=1, source_target_pairs={{0,2},{1,5},{2,0},{3,7},{4,6},{5,1},{6,4},{7,3},{8,10},{9,13},{10,... | collective-permute-start | bytes 688136 | tf_op jit(solution)/shard_map/ppermute | solution.py:27
  27.1 8.3 %collective-permute-start.7 = (bf16[64,1792]{1,0:T(8,128)(2,1)S(1)}, bf16[64,1792]{1,0:T(8,128)(2,1)S(1)}, u32[]{:S(2)}, u32[]{:S(2)}) collective-permute-start(bf16[64,1792]{1,0:T(8,128)(2,1)S(1)} %bitcast.109), channel_id=1, source_target_pairs={{0,2},{1,5},{2,0},{3,7},{4,6},{5,1},{6,4},{7,3},{8,10},{9,13},{10,... | collective-permute-start | bytes 688136 | tf_op jit(solution)/shard_map/ppermute | solution.py:27
  30.3 8.1 %collective-permute-start.2 = (bf16[64,1792]{1,0:T(8,128)(2,1)S(1)}, bf16[64,1792]{1,0:T(8,128)(2,1)S(1)}, u32[]{:S(2)}, u32[]{:S(2)}) collective-permute-start(bf16[64,1792]{1,0:T(8,128)(2,1)S(1)} %bitcast.111), channel_id=1, source_target_pairs={{0,2},{1,5},{2,0},{3,7},{4,6},{5,1},{6,4},{7,3},{8,10},{9,13},{10,... | collective-permute-start | bytes 688136 | tf_op jit(solution)/shard_map/ppermute | solution.py:27
  33.4 29.4 %collective-permute-start.28 = (bf16[96,3584]{1,0:T(8,128)(2,1)S(1)}, bf16[96,3584]{1,0:T(8,128)(2,1)S(1)}, u32[]{:S(2)}, u32[]{:S(2)}) collective-permute-start(bf16[96,3584]{1,0:T(8,128)(2,1)S(1)} %get-tuple-element.26), channel_id=1, source_target_pairs={{0,4},{1,3},{2,6},{3,1},{4,0},{5,7},{6,2},{7,5},{8,12},{9,11},{10,... | collective-permute-start | bytes 2064392 | tf_op jit(solution)/shard_map/ppermute | solution.py:27
  35.0 33.1 %collective-permute-start.29 = (bf16[96,3584]{1,0:T(8,128)(2,1)S(1)}, bf16[96,3584]{1,0:T(8,128)(2,1)S(1)}, u32[]{:S(2)}, u32[]{:S(2)}) collective-permute-start(bf16[96,3584]{1,0:T(8,128)(2,1)S(1)} %get-tuple-element.25), channel_id=1, source_target_pairs={{0,1},{1,0},{2,3},{3,2},{4,5},{5,4},{6,7},{7,6},{8,9},{9,8},{10,11... | collective-permute-start | bytes 2064392 | tf_op jit(solution)/shard_map/ppermute | solution.py:32
  35.8 16.5 %copy-start.1 = (bf16[1,1,3584,512]{3,2,1,0:T(8,128)(2,1)S(1)}, bf16[1,1,3584,512]{3,2,1,0:T(8,128)(2,1)}, u32[]{:S(2)}) copy-start(bf16[1,1,3584,512]{3,2,1,0:T(8,128)(2,1)} %param.18) | copy-start | bytes 11010052
  35.8 12.3 %collective-permute-start.8 = (bf16[96,1792]{1,0:T(8,128)(2,1)S(1)}, bf16[96,1792]{1,0:T(8,128)(2,1)S(1)}, u32[]{:S(2)}, u32[]{:S(2)}) collective-permute-start(bf16[96,1792]{1,0:T(8,128)(2,1)S(1)} %get-tuple-element.42), channel_id=1, source_target_pairs={{0,4},{1,3},{2,6},{3,1},{4,0},{5,7},{6,2},{7,5},{8,12},{9,11},{10,... | collective-permute-start | bytes 1032200 | tf_op jit(solution)/shard_map/ppermute | solution.py:27
  38.4 9.8 %collective-permute-start.9 = (bf16[96,1792]{1,0:T(8,128)(2,1)S(1)}, bf16[96,1792]{1,0:T(8,128)(2,1)S(1)}, u32[]{:S(2)}, u32[]{:S(2)}) collective-permute-start(bf16[96,1792]{1,0:T(8,128)(2,1)S(1)} %get-tuple-element.41), channel_id=1, source_target_pairs={{0,1},{1,0},{2,3},{3,2},{4,5},{5,4},{6,7},{7,6},{8,9},{9,8},{10,11... | collective-permute-start | bytes 1032200 | tf_op jit(solution)/shard_map/ppermute | solution.py:32
  38.8 13.0 %collective-permute-start.3 = (bf16[96,1792]{1,0:T(8,128)(2,1)S(1)}, bf16[96,1792]{1,0:T(8,128)(2,1)S(1)}, u32[]{:S(2)}, u32[]{:S(2)}) collective-permute-start(bf16[96,1792]{1,0:T(8,128)(2,1)S(1)} %get-tuple-element.40), channel_id=1, source_target_pairs={{0,4},{1,3},{2,6},{3,1},{4,0},{5,7},{6,2},{7,5},{8,12},{9,11},{10,... | collective-permute-start | bytes 1032200 | tf_op jit(solution)/shard_map/ppermute | solution.py:27
  48.1 3.7 %collective-permute-start.10 = (bf16[96,1792]{1,0:T(8,128)(2,1)S(1)}, bf16[96,1792]{1,0:T(8,128)(2,1)S(1)}, u32[]{:S(2)}, u32[]{:S(2)}) collective-permute-start(bf16[96,1792]{1,0:T(8,128)(2,1)S(1)} %collective-permute-done.8), channel_id=1, source_target_pairs={{0,1},{1,0},{2,3},{3,2},{4,5},{5,4},{6,7},{7,6},{8,9},{9,8},{10,11... | collective-permute-start | bytes 1032200 | tf_op jit(solution)/shard_map/ppermute | solution.py:32
  48.2 7.3 %collective-permute-start.24 = (bf16[96,1792]{1,0:T(8,128)(2,1)S(1)}, bf16[96,1792]{1,0:T(8,128)(2,1)S(1)}, u32[]{:S(2)}, u32[]{:S(2)}) collective-permute-start(bf16[96,1792]{1,0:T(8,128)(2,1)S(1)} %get-tuple-element.34), channel_id=1, source_target_pairs={{0,4},{1,3},{2,6},{3,1},{4,0},{5,7},{6,2},{7,5},{8,12},{9,11},{10,... | collective-permute-start | bytes 1032200 | tf_op jit(solution)/shard_map/ppermute | solution.py:27
  51.8 3.7 %collective-permute-start.4 = (bf16[96,1792]{1,0:T(8,128)(2,1)S(1)}, bf16[96,1792]{1,0:T(8,128)(2,1)S(1)}, u32[]{:S(2)}, u32[]{:S(2)}) collective-permute-start(bf16[96,1792]{1,0:T(8,128)(2,1)S(1)} %get-tuple-element.39), channel_id=1, source_target_pairs={{0,1},{1,0},{2,3},{3,2},{4,5},{5,4},{6,7},{7,6},{8,9},{9,8},{10,11... | collective-permute-start | bytes 1032200 | tf_op jit(solution)/shard_map/ppermute | solution.py:32
  51.8 5.3 %collective-permute-start.5 = (bf16[96,1792]{1,0:T(8,128)(2,1)S(1)}, bf16[96,1792]{1,0:T(8,128)(2,1)S(1)}, u32[]{:S(2)}, u32[]{:S(2)}) collective-permute-start(bf16[96,1792]{1,0:T(8,128)(2,1)S(1)} %collective-permute-done.3), channel_id=1, source_target_pairs={{0,1},{1,0},{2,3},{3,2},{4,5},{5,4},{6,7},{7,6},{8,9},{9,8},{10,11... | collective-permute-start | bytes 1032200 | tf_op jit(solution)/shard_map/ppermute | solution.py:32
  55.5 4.3 %collective-permute-start.25 = (bf16[96,1792]{1,0:T(8,128)(2,1)S(1)}, bf16[96,1792]{1,0:T(8,128)(2,1)S(1)}, u32[]{:S(2)}, u32[]{:S(2)}) collective-permute-start(bf16[96,1792]{1,0:T(8,128)(2,1)S(1)} %get-tuple-element.33), channel_id=1, source_target_pairs={{0,1},{1,0},{2,3},{3,2},{4,5},{5,4},{6,7},{7,6},{8,9},{9,8},{10,11... | collective-permute-start | bytes 1032200 | tf_op jit(solution)/shard_map/ppermute | solution.py:32
  55.5 2.5 %copy-start = (bf16[1,1,3584,512]{3,2,1,0:T(8,128)(2,1)S(1)}, bf16[1,1,3584,512]{3,2,1,0:T(8,128)(2,1)}, u32[]{:S(2)}) copy-start(bf16[1,1,3584,512]{3,2,1,0:T(8,128)(2,1)} %param.17) | copy-start | bytes 11010052
  55.5 7.3 %collective-permute-start.19 = (bf16[96,1792]{1,0:T(8,128)(2,1)S(1)}, bf16[96,1792]{1,0:T(8,128)(2,1)S(1)}, u32[]{:S(2)}, u32[]{:S(2)}) collective-permute-start(bf16[96,1792]{1,0:T(8,128)(2,1)S(1)} %get-tuple-element.32), channel_id=1, source_target_pairs={{0,4},{1,3},{2,6},{3,1},{4,0},{5,7},{6,2},{7,5},{8,12},{9,11},{10,... | collective-permute-start | bytes 1032200 | tf_op jit(solution)/shard_map/ppermute | solution.py:27
  57.1 6.2 %collective-permute-start.26 = (bf16[96,1792]{1,0:T(8,128)(2,1)S(1)}, bf16[96,1792]{1,0:T(8,128)(2,1)S(1)}, u32[]{:S(2)}, u32[]{:S(2)}) collective-permute-start(bf16[96,1792]{1,0:T(8,128)(2,1)S(1)} %collective-permute-done.24), channel_id=1, source_target_pairs={{0,1},{1,0},{2,3},{3,2},{4,5},{5,4},{6,7},{7,6},{8,9},{9,8},{10,11... | collective-permute-start | bytes 1032200 | tf_op jit(solution)/shard_map/ppermute | solution.py:32
  58.8 4.5 %copy-start.2 = (bf16[1,1,512,3584]{3,2,1,0:T(8,128)(2,1)S(1)}, bf16[1,1,512,3584]{3,2,1,0:T(8,128)(2,1)}, u32[]{:S(2)}) copy-start(bf16[1,1,512,3584]{3,2,1,0:T(8,128)(2,1)} %param.19) | copy-start | bytes 11010052
  59.7 4.5 %collective-permute-start.20 = (bf16[96,1792]{1,0:T(8,128)(2,1)S(1)}, bf16[96,1792]{1,0:T(8,128)(2,1)S(1)}, u32[]{:S(2)}, u32[]{:S(2)}) collective-permute-start(bf16[96,1792]{1,0:T(8,128)(2,1)S(1)} %get-tuple-element.31), channel_id=1, source_target_pairs={{0,1},{1,0},{2,3},{3,2},{4,5},{5,4},{6,7},{7,6},{8,9},{9,8},{10,11... | collective-permute-start | bytes 1032200 | tf_op jit(solution)/shard_map/ppermute | solution.py:32
  62.8 1.7 %collective-permute-start.21 = (bf16[96,1792]{1,0:T(8,128)(2,1)S(1)}, bf16[96,1792]{1,0:T(8,128)(2,1)S(1)}, u32[]{:S(2)}, u32[]{:S(2)}) collective-permute-start(bf16[96,1792]{1,0:T(8,128)(2,1)S(1)} %collective-permute-done.19), channel_id=1, source_target_pairs={{0,1},{1,0},{2,3},{3,2},{4,5},{5,4},{6,7},{7,6},{8,9},{9,8},{10,11... | collective-permute-start | bytes 1032200 | tf_op jit(solution)/shard_map/ppermute | solution.py:32
  62.8 5.3 %collective-permute-start.30 = (bf16[96,3584]{1,0:T(8,128)(2,1)S(1)}, bf16[96,3584]{1,0:T(8,128)(2,1)S(1)}, u32[]{:S(2)}, u32[]{:S(2)}) collective-permute-start(bf16[96,3584]{1,0:T(8,128)(2,1)S(1)} %collective-permute-done.28), channel_id=1, source_target_pairs={{0,1},{1,0},{2,3},{3,2},{4,5},{5,4},{6,7},{7,6},{8,9},{9,8},{10,11... | collective-permute-start | bytes 2064392 | tf_op jit(solution)/shard_map/ppermute | solution.py:32
  66.5 7.4 %collective-permute-start.11 = (bf16[192,1792]{1,0:T(8,128)(2,1)S(1)}, bf16[192,1792]{1,0:T(8,128)(2,1)S(1)}, u32[]{:S(2)}, u32[]{:S(2)}) collective-permute-start(bf16[192,1792]{1,0:T(8,128)(2,1)S(1)} %slice.222), channel_id=1, source_target_pairs={{0,1},{1,0},{2,3},{3,2},{4,5},{5,4},{6,7},{7,6},{8,9},{9,8},{10,11... | collective-permute-start | bytes 2064392 | tf_op jit(solution)/shard_map/ppermute | solution.py:32
  67.7 8.0 %collective-permute-start.14 = (bf16[192,1792]{1,0:T(8,128)(2,1)S(1)}, bf16[192,1792]{1,0:T(8,128)(2,1)S(1)}, u32[]{:S(2)}, u32[]{:S(2)}) collective-permute-start(bf16[192,1792]{1,0:T(8,128)(2,1)S(1)} %slice.229), channel_id=1, source_target_pairs={{0,1},{1,0},{2,3},{3,2},{4,5},{5,4},{6,7},{7,6},{8,9},{9,8},{10,11... | collective-permute-start | bytes 2064392 | tf_op jit(solution)/shard_map/ppermute | solution.py:32
  73.7 19.1 %collective-permute-start.31 = (bf16[192,1792]{1,0:T(8,128)(2,1)S(1)}, bf16[192,1792]{1,0:T(8,128)(2,1)S(1)}, u32[]{:S(2)}, u32[]{:S(2)}) collective-permute-start(bf16[192,1792]{1,0:T(8,128)(2,1)S(1)} %slice.241), channel_id=1, source_target_pairs={{0,1},{1,0},{2,3},{3,2},{4,5},{5,4},{6,7},{7,6},{8,9},{9,8},{10,11... | collective-permute-start | bytes 2064392 | tf_op jit(solution)/shard_map/ppermute | solution.py:32
  74.2 7.3 %collective-permute-start.12 = (bf16[96,1792]{1,0:T(8,128)(2,1)S(1)}, bf16[96,1792]{1,0:T(8,128)(2,1)S(1)}, u32[]{:S(2)}, u32[]{:S(2)}) collective-permute-start(bf16[96,1792]{1,0:T(8,128)(2,1)S(1)} %get-tuple-element.36), channel_id=1, source_target_pairs={{0,4},{1,3},{2,6},{3,1},{4,0},{5,7},{6,2},{7,5},{8,12},{9,11},{10,... | collective-permute-start | bytes 1032200 | tf_op jit(solution)/shard_map/ppermute | solution.py:27
  76.1 10.2 %collective-permute-start.15 = (bf16[96,1792]{1,0:T(8,128)(2,1)S(1)}, bf16[96,1792]{1,0:T(8,128)(2,1)S(1)}, u32[]{:S(2)}, u32[]{:S(2)}) collective-permute-start(bf16[96,1792]{1,0:T(8,128)(2,1)S(1)} %get-tuple-element.38), channel_id=1, source_target_pairs={{0,4},{1,3},{2,6},{3,1},{4,0},{5,7},{6,2},{7,5},{8,12},{9,11},{10,... | collective-permute-start | bytes 1032200 | tf_op jit(solution)/shard_map/ppermute | solution.py:27
  81.8 6.1 %collective-permute-start.13 = (bf16[64,1792]{1,0:T(8,128)(2,1)S(1)}, bf16[64,1792]{1,0:T(8,128)(2,1)S(1)}, u32[]{:S(2)}, u32[]{:S(2)}) collective-permute-start(bf16[64,1792]{1,0:T(8,128)(2,1)S(1)} %slice.226), channel_id=1, source_target_pairs={{0,2},{1,5},{2,0},{3,7},{4,6},{5,1},{6,4},{7,3},{8,10},{9,13},{10,... | collective-permute-start | bytes 688136 | tf_op jit(solution)/shard_map/ppermute | solution.py:27
  83.7 10.9 %collective-permute-start.34 = (bf16[192,1792]{1,0:T(8,128)(2,1)S(1)}, bf16[192,1792]{1,0:T(8,128)(2,1)S(1)}, u32[]{:S(2)}, u32[]{:S(2)}) collective-permute-start(bf16[192,1792]{1,0:T(8,128)(2,1)S(1)} %slice.247), channel_id=1, source_target_pairs={{0,1},{1,0},{2,3},{3,2},{4,5},{5,4},{6,7},{7,6},{8,9},{9,8},{10,11... | collective-permute-start | bytes 2064392 | tf_op jit(solution)/shard_map/ppermute | solution.py:32
  86.7 6.1 %collective-permute-start.16 = (bf16[64,1792]{1,0:T(8,128)(2,1)S(1)}, bf16[64,1792]{1,0:T(8,128)(2,1)S(1)}, u32[]{:S(2)}, u32[]{:S(2)}) collective-permute-start(bf16[64,1792]{1,0:T(8,128)(2,1)S(1)} %slice.233), channel_id=1, source_target_pairs={{0,2},{1,5},{2,0},{3,7},{4,6},{5,1},{6,4},{7,3},{8,10},{9,13},{10,... | collective-permute-start | bytes 688136 | tf_op jit(solution)/shard_map/ppermute | solution.py:27
  93.0 8.2 %collective-permute-start.32 = (bf16[96,1792]{1,0:T(8,128)(2,1)S(1)}, bf16[96,1792]{1,0:T(8,128)(2,1)S(1)}, u32[]{:S(2)}, u32[]{:S(2)}) collective-permute-start(bf16[96,1792]{1,0:T(8,128)(2,1)S(1)} %get-tuple-element.28), channel_id=1, source_target_pairs={{0,4},{1,3},{2,6},{3,1},{4,0},{5,7},{6,2},{7,5},{8,12},{9,11},{10,... | collective-permute-start | bytes 1032200 | tf_op jit(solution)/shard_map/ppermute | solution.py:27
  94.9 13.8 %collective-permute-start.35 = (bf16[96,1792]{1,0:T(8,128)(2,1)S(1)}, bf16[96,1792]{1,0:T(8,128)(2,1)S(1)}, u32[]{:S(2)}, u32[]{:S(2)}) collective-permute-start(bf16[96,1792]{1,0:T(8,128)(2,1)S(1)} %get-tuple-element.30), channel_id=1, source_target_pairs={{0,4},{1,3},{2,6},{3,1},{4,0},{5,7},{6,2},{7,5},{8,12},{9,11},{10,... | collective-permute-start | bytes 1032200 | tf_op jit(solution)/shard_map/ppermute | solution.py:27
  101.6 8.1 %collective-permute-start.33 = (bf16[64,1792]{1,0:T(8,128)(2,1)S(1)}, bf16[64,1792]{1,0:T(8,128)(2,1)S(1)}, u32[]{:S(2)}, u32[]{:S(2)}) collective-permute-start(bf16[64,1792]{1,0:T(8,128)(2,1)S(1)} %slice.245), channel_id=1, source_target_pairs={{0,2},{1,5},{2,0},{3,7},{4,6},{5,1},{6,4},{7,3},{8,10},{9,13},{10,... | collective-permute-start | bytes 688136 | tf_op jit(solution)/shard_map/ppermute | solution.py:27
  109.0 6.1 %collective-permute-start.36 = (bf16[64,1792]{1,0:T(8,128)(2,1)S(1)}, bf16[64,1792]{1,0:T(8,128)(2,1)S(1)}, u32[]{:S(2)}, u32[]{:S(2)}) collective-permute-start(bf16[64,1792]{1,0:T(8,128)(2,1)S(1)} %slice.251), channel_id=1, source_target_pairs={{0,2},{1,5},{2,0},{3,7},{4,6},{5,1},{6,4},{7,3},{8,10},{9,13},{10,... | collective-permute-start | bytes 688136 | tf_op jit(solution)/shard_map/ppermute | solution.py:27
where the time goes:
time: 116 us
  waiting for transfers between devices  54.3 us (47%)
  starting transfers between devices  32.8 us (28%)
  matrix products  18.8 us (16%)
  other arithmetic  6.08 us (5%)
  local copies, waits for them, and re-layouts  2.89 us (2%)
    ppermute x19, waiting for transfers between devices, exchange(): return lax.ppermute(block, 'expert', route)  44 us
    ppermute x19, starting transfers between devices, exchange(): return lax.ppermute(block, 'expert', route)  23.9 us
    dot_general x13, matrix products, matmul(): return jnp.dot(left, right, preferred_element_type=jnp.float32)  11.3 us
    ppermute x4, waiting for transfers between devices, shift(): lax.ppermute(block, axis, [((i - distance) % count, i) for i in range(cou...  10.1 us
    ppermute x4, starting transfers between devices, shift(): lax.ppermute(block, axis, [((i - distance) % count, i) for i in range(cou...  6.29 us
    dot_general x6, matrix products, contract_last(): lax.dot_general(left, right, (((1,), (1,)), ((), ())), preferred_element_...  5.43 us
    ppermute x14, starting transfers between devices, swap_cores(): return lax.ppermute(block, 'expert', [(i, i ^ 1) for i in range(count)])  2.52 us
  transfers between devices with their start and end apart: 37, of which 17 were waited for; matrix products, arithmetic and copies ran while one was open for 22% of the time, Pallas kernels for 0%

commit v1 on v0

--- a/solution.py
+++ b/solution.py
@@ -83,6 +83,7 @@
 
 
 PARTS = {"x": 1, "g": 2, "a": 2, "rb": 2, "ra": 2}
+EARLY = False
 
 
 def pieces(block, count):
@@ -150,10 +151,14 @@
         0,
     )
 
-    def deliver(raw, onehot, scale=None):
+    def deliver(raw, onehot, name, scale=None):
         out = []
         for x in raw:
-            picked = matmul(onehot, x)
+            if EARLY and name == "x":
+                picked = lax.optimization_barrier(matmul(onehot[:, :tok_rows], x[:tok_rows]))
+                picked = matmul(onehot[:, tok_rows:], x[tok_rows:]) + picked
+            else:
+                picked = matmul(onehot, x)
             picked = (picked if scale is None else picked * scale).astype(jnp.bfloat16)
             mine, theirs = picked[:held], picked[held:]
             got = last_exchange(theirs)
@@ -162,9 +167,9 @@
             out.append(jnp.concatenate([mine, got, mine_there, got_there], 0))
         return out
 
-    rows_x = deliver(raw_b, onehot_b)
-    rows_g = deliver([gather(x, 0) for x in upstream], onehot_b, scale_b)
-    rows_a = deliver([gather(x, 0) for x in incoming], onehot_a)
+    rows_x = deliver(raw_b, onehot_b, "x")
+    rows_g = deliver([gather(x, 0) for x in upstream], onehot_b, "g", scale_b)
+    rows_a = deliver([gather(x, 0) for x in incoming], onehot_a, "a")
 
     def give_back(parts, spread):
         out = []

time: 116 us -> 116 us (level)
  no operation moved by 1% of the time
where the time goes in v1:
time: 116 us
  waiting for transfers between devices  54.3 us (47%)
  starting transfers between devices  32.8 us (28%)
  matrix products  18.8 us (16%)
  other arithmetic  6.08 us (5%)
  local copies, waits for them, and re-layouts  2.89 us (2%)
    ppermute x19, waiting for transfers between devices, exchange(): return lax.ppermute(block, 'expert', route)  44 us
    ppermute x19, starting transfers between devices, exchange(): return lax.ppermute(block, 'expert', route)  23.9 us
    dot_general x13, matrix products, matmul(): return jnp.dot(left, right, preferred_element_type=jnp.float32)  11.3 us
    ppermute x4, waiting for transfers between devices, shift(): lax.ppermute(block, axis, [((i - distance) % count, i) for i in range(cou...  10.1 us
    ppermute x4, starting transfers between devices, shift(): lax.ppermute(block, axis, [((i - distance) % count, i) for i in range(cou...  6.29 us
    dot_general x6, matrix products, contract_last(): lax.dot_general(left, right, (((1,), (1,)), ((), ())), preferred_element_...  5.43 us
    ppermute x14, starting transfers between devices, swap_cores(): return lax.ppermute(block, 'expert', [(i, i ^ 1) for i in range(count)])  2.52 us
  transfers between devices with their start and end apart: 37, of which 17 were waited for; matrix products, arithmetic and copies ran while one was open for 22% of the time, Pallas kernels for 0%

profile of v1, /device:TPU:0, one launch (start us, length us, event | category | flops | bytes accessed | tf_op | source)
XLA Modules:
  0.0 115.9 jit_solution(16907178924029464191)
XLA Ops:
  0.6 0.7 convert_bitcast_fusion
  1.3 0.7 pad_maximum_fusion.12
  2.0 3.0 %collective-permute-start = (f32[8,64]{1,0:T(8,128)S(1)}, f32[8,64]{1,0:T(8,128)S(1)}, u32[]{:S(2)}, u32[]{:S(2)}) collective-permute-start(f32[8,64]{1,0:T(8,128)S(1)} %pad_maximum_fusion.12), channel_id=1, source_target_pairs={{0,2},{1,5},{2,0},{3,7},{4,6},{5,1},{6,4},{7,3},{8,10},{9,13},{10,... | collective-permute-start | bytes 6152 | tf_op jit(solution)/shard_map/ppermute | solution.py:27
  5.1 1.1 fusion.141
  6.2 4.1 %collective-permute-start.22 = (bf16[1,64,1792]{2,1,0:T(8,128)(2,1)S(1)}, bf16[1,64,1792]{2,1,0:T(8,128)(2,1)S(1)}, u32[]{:S(2)}, u32[]{:S(2)}) collective-permute-start(bf16[1,64,1792]{2,1,0:T(8,128)(2,1)S(1)} %get-tuple-element.44), channel_id=1, source_target_pairs={{8,0},{16,8},{24,16},{0,24},{9,1},{17,9},{25,17},{1,25},{10,2},{18... | collective-permute-start | bytes 688136 | tf_op jit(solution)/shard_map/ppermute | solution.py:9
  10.3 0.4 collective-permute-start.17
  10.8 1.1 fusion.142
  11.9 1.6 %collective-permute-start.6 = (bf16[1,64,1792]{2,1,0:T(8,128)(2,1)S(1)}, bf16[1,64,1792]{2,1,0:T(8,128)(2,1)S(1)}, u32[]{:S(2)}, u32[]{:S(2)}) collective-permute-start(bf16[1,64,1792]{2,1,0:T(8,128)(2,1)S(1)} %get-tuple-element.46), channel_id=1, source_target_pairs={{24,0},{0,8},{8,16},{16,24},{25,1},{1,9},{9,17},{17,25},{26,2},{2,... | collective-permute-start | bytes 688136 | tf_op jit(solution)/shard_map/ppermute | solution.py:9
  13.6 0.8 pad_maximum_fusion.13
  15.7 0.7 collective-permute-done.22
  16.4 1.5 %collective-permute-start.23 = (bf16[64,1792]{1,0:T(8,128)(2,1)S(1)}, bf16[64,1792]{1,0:T(8,128)(2,1)S(1)}, u32[]{:S(2)}, u32[]{:S(2)}) collective-permute-start(bf16[64,1792]{1,0:T(8,128)(2,1)S(1)} %bitcast.127), channel_id=1, source_target_pairs={{0,2},{1,5},{2,0},{3,7},{4,6},{5,1},{6,4},{7,3},{8,10},{9,13},{10,... | collective-permute-start | bytes 688136 | tf_op jit(solution)/shard_map/ppermute | solution.py:27
  17.9 3.4 %collective-permute-done.17 = bf16[1,64,1792]{2,1,0:T(8,128)(2,1)S(1)} collective-permute-done((bf16[1,64,1792]{2,1,0:T(8,128)(2,1)S(1)}, bf16[1,64,1792]{2,1,0:T(8,128)(2,1)S(1)}, u32[]{:S(2)}, u32[]{:S(2)}) %collective-permute-start.17) | collective-permute-done | bytes 229408 | tf_op jit(solution)/shard_map/ppermute | solution.py:9
  21.3 1.5 %collective-permute-start.18 = (bf16[64,1792]{1,0:T(8,128)(2,1)S(1)}, bf16[64,1792]{1,0:T(8,128)(2,1)S(1)}, u32[]{:S(2)}, u32[]{:S(2)}) collective-permute-start(bf16[64,1792]{1,0:T(8,128)(2,1)S(1)} %bitcast.125), channel_id=1, source_target_pairs={{0,2},{1,5},{2,0},{3,7},{4,6},{5,1},{6,4},{7,3},{8,10},{9,13},{10,... | collective-permute-start | bytes 688136 | tf_op jit(solution)/shard_map/ppermute | solution.py:27
  22.8 4.2 %collective-permute-done.6 = bf16[1,64,1792]{2,1,0:T(8,128)(2,1)S(1)} collective-permute-done((bf16[1,64,1792]{2,1,0:T(8,128)(2,1)S(1)}, bf16[1,64,1792]{2,1,0:T(8,128)(2,1)S(1)}, u32[]{:S(2)}, u32[]{:S(2)}) %collective-permute-start.6) | collective-permute-done | bytes 229408 | tf_op jit(solution)/shard_map/ppermute | solution.py:9
  27.1 1.5 %collective-permute-start.7 = (bf16[64,1792]{1,0:T(8,128)(2,1)S(1)}, bf16[64,1792]{1,0:T(8,128)(2,1)S(1)}, u32[]{:S(2)}, u32[]{:S(2)}) collective-permute-start(bf16[64,1792]{1,0:T(8,128)(2,1)S(1)} %bitcast.109), channel_id=1, source_target_pairs={{0,2},{1,5},{2,0},{3,7},{4,6},{5,1},{6,4},{7,3},{8,10},{9,13},{10,... | collective-permute-start | bytes 688136 | tf_op jit(solution)/shard_map/ppermute | solution.py:27
  28.6 1.7 %collective-permute-done.1 = bf16[1,64,1792]{2,1,0:T(8,128)(2,1)S(1)} collective-permute-done((bf16[1,64,1792]{2,1,0:T(8,128)(2,1)S(1)}, bf16[1,64,1792]{2,1,0:T(8,128)(2,1)S(1)}, u32[]{:S(2)}, u32[]{:S(2)}) %collective-permute-start.1) | collective-permute-done | bytes 229408 | tf_op jit(solution)/shard_map/ppermute | solution.py:9
  30.3 1.5 %collective-permute-start.2 = (bf16[64,1792]{1,0:T(8,128)(2,1)S(1)}, bf16[64,1792]{1,0:T(8,128)(2,1)S(1)}, u32[]{:S(2)}, u32[]{:S(2)}) collective-permute-start(bf16[64,1792]{1,0:T(8,128)(2,1)S(1)} %bitcast.111), channel_id=1, source_target_pairs={{0,2},{1,5},{2,0},{3,7},{4,6},{5,1},{6,4},{7,3},{8,10},{9,13},{10,... | collective-permute-start | bytes 688136 | tf_op jit(solution)/shard_map/ppermute | solution.py:27
  31.8 1.5 %convolution_convert_fusion = bf16[192,3584]{1,0:T(8,128)(2,1)S(1)} fusion(bf16[64,3584]{1,0:T(8,128)(2,1)S(1)} %collective-permute-done.27, bf16[64,3584]{1,0:T(8,128)(2,1)} %bitcast.108, pred[96,128]{1,0:T(32,128)(4,1)S(1)} %iota_compare_fusion.1, pred[96,128]{1,0:T(32,128)(4,1)S(1)} %iota_compare_fusion.2), kind=kOutput, calls=%fused_computation | convolution fusion | flops 178708480 | bytes 2318336 | tf_op jit(solution)/shard_map/dot_general | solution.py:74
  33.4 1.6 %collective-permute-start.28 = (bf16[96,3584]{1,0:T(8,128)(2,1)S(1)}, bf16[96,3584]{1,0:T(8,128)(2,1)S(1)}, u32[]{:S(2)}, u32[]{:S(2)}) collective-permute-start(bf16[96,3584]{1,0:T(8,128)(2,1)S(1)} %get-tuple-element.26), channel_id=1, source_target_pairs={{0,4},{1,3},{2,6},{3,1},{4,0},{5,7},{6,2},{7,5},{8,12},{9,11},{10,... | collective-permute-start | bytes 2064392 | tf_op jit(solution)/shard_map/ppermute | solution.py:27
  35.8 0.6 collective-permute-start.8
  36.4 2.0 %collective-permute-done.2 = bf16[64,1792]{1,0:T(8,128)(2,1)S(1)} collective-permute-done((bf16[64,1792]{1,0:T(8,128)(2,1)S(1)}, bf16[64,1792]{1,0:T(8,128)(2,1)S(1)}, u32[]{:S(2)}, u32[]{:S(2)}) %collective-permute-start.2) | collective-permute-done | bytes 229408 | tf_op jit(solution)/shard_map/ppermute | solution.py:27
  38.8 2.0 %collective-permute-start.3 = (bf16[96,1792]{1,0:T(8,128)(2,1)S(1)}, bf16[96,1792]{1,0:T(8,128)(2,1)S(1)}, u32[]{:S(2)}, u32[]{:S(2)}) collective-permute-start(bf16[96,1792]{1,0:T(8,128)(2,1)S(1)} %get-tuple-element.40), channel_id=1, source_target_pairs={{0,4},{1,3},{2,6},{3,1},{4,0},{5,7},{6,2},{7,5},{8,12},{9,11},{10,... | collective-permute-start | bytes 1032200 | tf_op jit(solution)/shard_map/ppermute | solution.py:27
  41.1 7.0 %collective-permute-done.8 = bf16[96,1792]{1,0:T(8,128)(2,1)S(1)} collective-permute-done((bf16[96,1792]{1,0:T(8,128)(2,1)S(1)}, bf16[96,1792]{1,0:T(8,128)(2,1)S(1)}, u32[]{:S(2)}, u32[]{:S(2)}) %collective-permute-start.8) | collective-permute-done | bytes 344096 | tf_op jit(solution)/shard_map/ppermute | solution.py:27
  48.2 1.6 %collective-permute-start.24 = (bf16[96,1792]{1,0:T(8,128)(2,1)S(1)}, bf16[96,1792]{1,0:T(8,128)(2,1)S(1)}, u32[]{:S(2)}, u32[]{:S(2)}) collective-permute-start(bf16[96,1792]{1,0:T(8,128)(2,1)S(1)} %get-tuple-element.34), channel_id=1, source_target_pairs={{0,4},{1,3},{2,6},{3,1},{4,0},{5,7},{6,2},{7,5},{8,12},{9,11},{10,... | collective-permute-start | bytes 1032200 | tf_op jit(solution)/shard_map/ppermute | solution.py:27
  49.7 2.0 %collective-permute-done.3 = bf16[96,1792]{1,0:T(8,128)(2,1)S(1)} collective-permute-done((bf16[96,1792]{1,0:T(8,128)(2,1)S(1)}, bf16[96,1792]{1,0:T(8,128)(2,1)S(1)}, u32[]{:S(2)}, u32[]{:S(2)}) %collective-permute-start.3) | collective-permute-done | bytes 344096 | tf_op jit(solution)/shard_map/ppermute | solution.py:27
  51.8 0.5 collective-permute-start.5
  52.3 0.9 fusion.9
  53.2 2.3 %collective-permute-done.24 = bf16[96,1792]{1,0:T(8,128)(2,1)S(1)} collective-permute-done((bf16[96,1792]{1,0:T(8,128)(2,1)S(1)}, bf16[96,1792]{1,0:T(8,128)(2,1)S(1)}, u32[]{:S(2)}, u32[]{:S(2)}) %collective-permute-start.24) | collective-permute-done | bytes 344096 | tf_op jit(solution)/shard_map/ppermute | solution.py:27
  55.5 1.6 %collective-permute-start.19 = (bf16[96,1792]{1,0:T(8,128)(2,1)S(1)}, bf16[96,1792]{1,0:T(8,128)(2,1)S(1)}, u32[]{:S(2)}, u32[]{:S(2)}) collective-permute-start(bf16[96,1792]{1,0:T(8,128)(2,1)S(1)} %get-tuple-element.32), channel_id=1, source_target_pairs={{0,4},{1,3},{2,6},{3,1},{4,0},{5,7},{6,2},{7,5},{8,12},{9,11},{10,... | collective-permute-start | bytes 1032200 | tf_op jit(solution)/shard_map/ppermute | solution.py:27
  57.1 0.9 fusion.53
  58.0 0.9 fusion.16
  58.8 0.9 fusion.50
  59.7 0.6 collective-permute-start.20
  60.3 2.5 %collective-permute-done.19 = bf16[96,1792]{1,0:T(8,128)(2,1)S(1)} collective-permute-done((bf16[96,1792]{1,0:T(8,128)(2,1)S(1)}, bf16[96,1792]{1,0:T(8,128)(2,1)S(1)}, u32[]{:S(2)}, u32[]{:S(2)}) %collective-permute-start.19) | collective-permute-done | bytes 344096 | tf_op jit(solution)/shard_map/ppermute | solution.py:27
  62.8 0.5 collective-permute-start.30
  63.3 0.9 fusion.25
  64.5 0.9 fusion.56
  65.6 0.9 convolution_convert_fusion.2
  66.7 0.9 convolution_convert_fusion.1
  67.7 0.4 collective-permute-start.14
  68.1 1.6 %fusion = f32[384,512]{1,0:T(8,128)S(1)} fusion(bf16[1,1,3584,512]{3,2,1,0:T(8,128)(2,1)S(1)} %copy-done.1, bf16[96,3584]{1,0:T(8,128)(2,1)S(1)} %collective-permute-done.30, bf16[96,3584]{1,0:T(8,128)(2,1)S(1)} %collective-permute-done.29, bf16[96,3584]{1,0:T(8,128)(2,1)S(1)} %collective-permute-done.28, bf16[96,3584]{1,0:T(8,128)(2,1)S(1)} %get-tuple-element.25), kind=kOutput, calls=%fused_computation.1 | convolution fusion | flops 1420296192 | bytes 7208960 | tf_op jit(solution)/shard_map/dot_general | solution.py:74
  69.7 1.6 %fusion.2 = f32[384,512]{1,0:T(8,128)S(1)} fusion(bf16[1,1,3584,512]{3,2,1,0:T(8,128)(2,1)S(1)} %copy-done, bf16[96,3584]{1,0:T(8,128)(2,1)S(1)} %collective-permute-done.30, bf16[96,3584]{1,0:T(8,128)(2,1)S(1)} %collective-permute-done.29, bf16[96,3584]{1,0:T(8,128)(2,1)S(1)} %collective-permute-done.28, bf16[96,3584]{1,0:T(8,128)(2,1)S(1)} %get-tuple-element.25), kind=kOutput, calls=%fused_computation.3 | convolution fusion | flops 1420296192 | bytes 7208960 | tf_op jit(solution)/shard_map/dot_general | solution.py:74
  71.3 0.5 multiply_convert_fusion
  71.9 0.9 fusion.14
  72.8 0.9 fusion.4
  74.2 1.6 %collective-permute-start.12 = (bf16[96,1792]{1,0:T(8,128)(2,1)S(1)}, bf16[96,1792]{1,0:T(8,128)(2,1)S(1)}, u32[]{:S(2)}, u32[]{:S(2)}) collective-permute-start(bf16[96,1792]{1,0:T(8,128)(2,1)S(1)} %get-tuple-element.36), channel_id=1, source_target_pairs={{0,4},{1,3},{2,6},{3,1},{4,0},{5,7},{6,2},{7,5},{8,12},{9,11},{10,... | collective-permute-start | bytes 1032200 | tf_op jit(solution)/shard_map/ppermute | solution.py:27
  75.7 0.3 add_convert_fusion.2
  76.1 0.6 collective-permute-start.15
  76.7 0.9 fusion.18
  77.6 3.8 %collective-permute-done.12 = bf16[96,1792]{1,0:T(8,128)(2,1)S(1)} collective-permute-done((bf16[96,1792]{1,0:T(8,128)(2,1)S(1)}, bf16[96,1792]{1,0:T(8,128)(2,1)S(1)}, u32[]{:S(2)}, u32[]{:S(2)}) %collective-permute-start.12) | collective-permute-done | bytes 344096 | tf_op jit(solution)/shard_map/ppermute | solution.py:27
  81.8 0.9 collective-permute-start.13
  82.7 0.9 fusion.5
  83.8 2.5 %collective-permute-done.15 = bf16[96,1792]{1,0:T(8,128)(2,1)S(1)} collective-permute-done((bf16[96,1792]{1,0:T(8,128)(2,1)S(1)}, bf16[96,1792]{1,0:T(8,128)(2,1)S(1)}, u32[]{:S(2)}, u32[]{:S(2)}) %collective-permute-start.15) | collective-permute-done | bytes 344096 | tf_op jit(solution)/shard_map/ppermute | solution.py:27
  86.7 0.9 collective-permute-start.16
  88.0 4.8 %collective-permute-done.16 = bf16[64,1792]{1,0:T(8,128)(2,1)S(1)} collective-permute-done((bf16[64,1792]{1,0:T(8,128)(2,1)S(1)}, bf16[64,1792]{1,0:T(8,128)(2,1)S(1)}, u32[]{:S(2)}, u32[]{:S(2)}) %collective-permute-start.16) | collective-permute-done | bytes 229408 | tf_op jit(solution)/shard_map/ppermute | solution.py:27
  93.0 1.6 %collective-permute-start.32 = (bf16[96,1792]{1,0:T(8,128)(2,1)S(1)}, bf16[96,1792]{1,0:T(8,128)(2,1)S(1)}, u32[]{:S(2)}, u32[]{:S(2)}) collective-permute-start(bf16[96,1792]{1,0:T(8,128)(2,1)S(1)} %get-tuple-element.28), channel_id=1, source_target_pairs={{0,4},{1,3},{2,6},{3,1},{4,0},{5,7},{6,2},{7,5},{8,12},{9,11},{10,... | collective-permute-start | bytes 1032200 | tf_op jit(solution)/shard_map/ppermute | solution.py:27
  94.9 0.6 collective-permute-start.35
  95.4 5.8 %collective-permute-done.32 = bf16[96,1792]{1,0:T(8,128)(2,1)S(1)} collective-permute-done((bf16[96,1792]{1,0:T(8,128)(2,1)S(1)}, bf16[96,1792]{1,0:T(8,128)(2,1)S(1)}, u32[]{:S(2)}, u32[]{:S(2)}) %collective-permute-start.32) | collective-permute-done | bytes 344096 | tf_op jit(solution)/shard_map/ppermute | solution.py:27
  101.6 0.7 collective-permute-start.33
  102.3 0.8 maximum_bitcast_fusion
  103.1 5.5 %collective-permute-done.35 = bf16[96,1792]{1,0:T(8,128)(2,1)S(1)} collective-permute-done((bf16[96,1792]{1,0:T(8,128)(2,1)S(1)}, bf16[96,1792]{1,0:T(8,128)(2,1)S(1)}, u32[]{:S(2)}, u32[]{:S(2)}) %collective-permute-start.35) | collective-permute-done | bytes 344096 | tf_op jit(solution)/shard_map/ppermute | solution.py:27
  109.0 0.7 collective-permute-start.36
  109.8 5.3 %collective-permute-done.36 = bf16[64,1792]{1,0:T(8,128)(2,1)S(1)} collective-permute-done((bf16[64,1792]{1,0:T(8,128)(2,1)S(1)}, bf16[64,1792]{1,0:T(8,128)(2,1)S(1)}, u32[]{:S(2)}, u32[]{:S(2)}) %collective-permute-start.36) | collective-permute-done | bytes 229408 | tf_op jit(solution)/shard_map/ppermute | solution.py:27
  115.1 0.8 maximum_bitcast_fusion.1
  (91 shorter events, 6.8 us)
Async XLA Ops:
  2.0 11.5 %collective-permute-start = (f32[8,64]{1,0:T(8,128)S(1)}, f32[8,64]{1,0:T(8,128)S(1)}, u32[]{:S(2)}, u32[]{:S(2)}) collective-permute-start(f32[8,64]{1,0:T(8,128)S(1)} %pad_maximum_fusion.12), channel_id=1, source_target_pairs={{0,2},{1,5},{2,0},{3,7},{4,6},{5,1},{6,4},{7,3},{8,10},{9,13},{10,... | collective-permute-start | bytes 6152 | tf_op jit(solution)/shard_map/ppermute | solution.py:27
  5.1 26.7 %collective-permute-start.27 = (bf16[64,3584]{1,0:T(8,128)(2,1)}, bf16[64,3584]{1,0:T(8,128)(2,1)S(1)}, u32[]{:S(2)}, u32[]{:S(2)}) collective-permute-start(bf16[64,3584]{1,0:T(8,128)(2,1)} %bitcast.107), channel_id=1, source_target_pairs={{0,2},{1,5},{2,0},{3,7},{4,6},{5,1},{6,4},{7,3},{8,10},{9,13},{10,... | collective-permute-start | bytes 1376264 | tf_op jit(solution)/shard_map/ppermute | solution.py:27
  6.2 10.2 %collective-permute-start.22 = (bf16[1,64,1792]{2,1,0:T(8,128)(2,1)S(1)}, bf16[1,64,1792]{2,1,0:T(8,128)(2,1)S(1)}, u32[]{:S(2)}, u32[]{:S(2)}) collective-permute-start(bf16[1,64,1792]{2,1,0:T(8,128)(2,1)S(1)} %get-tuple-element.44), channel_id=1, source_target_pairs={{8,0},{16,8},{24,16},{0,24},{9,1},{17,9},{25,17},{1,25},{10,2},{18... | collective-permute-start | bytes 688136 | tf_op jit(solution)/shard_map/ppermute | solution.py:9
  10.3 11.0 %collective-permute-start.17 = (bf16[1,64,1792]{2,1,0:T(8,128)(2,1)S(1)}, bf16[1,64,1792]{2,1,0:T(8,128)(2,1)S(1)}, u32[]{:S(2)}, u32[]{:S(2)}) collective-permute-start(bf16[1,64,1792]{2,1,0:T(8,128)(2,1)S(1)} %get-tuple-element.43), channel_id=1, source_target_pairs={{8,0},{16,8},{24,16},{0,24},{9,1},{17,9},{25,17},{1,25},{10,2},{18... | collective-permute-start | bytes 688136 | tf_op jit(solution)/shard_map/ppermute | solution.py:9
  11.9 15.2 %collective-permute-start.6 = (bf16[1,64,1792]{2,1,0:T(8,128)(2,1)S(1)}, bf16[1,64,1792]{2,1,0:T(8,128)(2,1)S(1)}, u32[]{:S(2)}, u32[]{:S(2)}) collective-permute-start(bf16[1,64,1792]{2,1,0:T(8,128)(2,1)S(1)} %get-tuple-element.46), channel_id=1, source_target_pairs={{24,0},{0,8},{8,16},{16,24},{25,1},{1,9},{9,17},{17,25},{26,2},{2,... | collective-permute-start | bytes 688136 | tf_op jit(solution)/shard_map/ppermute | solution.py:9
  13.5 16.8 %collective-permute-start.1 = (bf16[1,64,1792]{2,1,0:T(8,128)(2,1)S(1)}, bf16[1,64,1792]{2,1,0:T(8,128)(2,1)S(1)}, u32[]{:S(2)}, u32[]{:S(2)}) collective-permute-start(bf16[1,64,1792]{2,1,0:T(8,128)(2,1)S(1)} %get-tuple-element.45), channel_id=1, source_target_pairs={{24,0},{0,8},{8,16},{16,24},{25,1},{1,9},{9,17},{17,25},{26,2},{2,... | collective-permute-start | bytes 688136 | tf_op jit(solution)/shard_map/ppermute | solution.py:9
  16.4 18.6 %collective-permute-start.23 = (bf16[64,1792]{1,0:T(8,128)(2,1)S(1)}, bf16[64,1792]{1,0:T(8,128)(2,1)S(1)}, u32[]{:S(2)}, u32[]{:S(2)}) collective-permute-start(bf16[64,1792]{1,0:T(8,128)(2,1)S(1)} %bitcast.127), channel_id=1, source_target_pairs={{0,2},{1,5},{2,0},{3,7},{4,6},{5,1},{6,4},{7,3},{8,10},{9,13},{10,... | collective-permute-start | bytes 688136 | tf_op jit(solution)/shard_map/ppermute | solution.py:27
  21.3 17.4 %collective-permute-start.18 = (bf16[64,1792]{1,0:T(8,128)(2,1)S(1)}, bf16[64,1792]{1,0:T(8,128)(2,1)S(1)}, u32[]{:S(2)}, u32[]{:S(2)}) collective-permute-start(bf16[64,1792]{1,0:T(8,128)(2,1)S(1)} %bitcast.125), channel_id=1, source_target_pairs={{0,2},{1,5},{2,0},{3,7},{4,6},{5,1},{6,4},{7,3},{8,10},{9,13},{10,... | collective-permute-start | bytes 688136 | tf_op jit(solution)/shard_map/ppermute | solution.py:27
  27.1 8.3 %collective-permute-start.7 = (bf16[64,1792]{1,0:T(8,128)(2,1)S(1)}, bf16[64,1792]{1,0:T(8,128)(2,1)S(1)}, u32[]{:S(2)}, u32[]{:S(2)}) collective-permute-start(bf16[64,1792]{1,0:T(8,128)(2,1)S(1)} %bitcast.109), channel_id=1, source_target_pairs={{0,2},{1,5},{2,0},{3,7},{4,6},{5,1},{6,4},{7,3},{8,10},{9,13},{10,... | collective-permute-start | bytes 688136 | tf_op jit(solution)/shard_map/ppermute | solution.py:27
  30.3 8.1 %collective-permute-start.2 = (bf16[64,1792]{1,0:T(8,128)(2,1)S(1)}, bf16[64,1792]{1,0:T(8,128)(2,1)S(1)}, u32[]{:S(2)}, u32[]{:S(2)}) collective-permute-start(bf16[64,1792]{1,0:T(8,128)(2,1)S(1)} %bitcast.111), channel_id=1, source_target_pairs={{0,2},{1,5},{2,0},{3,7},{4,6},{5,1},{6,4},{7,3},{8,10},{9,13},{10,... | collective-permute-start | bytes 688136 | tf_op jit(solution)/shard_map/ppermute | solution.py:27
  33.4 29.4 %collective-permute-start.28 = (bf16[96,3584]{1,0:T(8,128)(2,1)S(1)}, bf16[96,3584]{1,0:T(8,128)(2,1)S(1)}, u32[]{:S(2)}, u32[]{:S(2)}) collective-permute-start(bf16[96,3584]{1,0:T(8,128)(2,1)S(1)} %get-tuple-element.26), channel_id=1, source_target_pairs={{0,4},{1,3},{2,6},{3,1},{4,0},{5,7},{6,2},{7,5},{8,12},{9,11},{10,... | collective-permute-start | bytes 2064392 | tf_op jit(solution)/shard_map/ppermute | solution.py:27
  35.0 33.1 %collective-permute-start.29 = (bf16[96,3584]{1,0:T(8,128)(2,1)S(1)}, bf16[96,3584]{1,0:T(8,128)(2,1)S(1)}, u32[]{:S(2)}, u32[]{:S(2)}) collective-permute-start(bf16[96,3584]{1,0:T(8,128)(2,1)S(1)} %get-tuple-element.25), channel_id=1, source_target_pairs={{0,1},{1,0},{2,3},{3,2},{4,5},{5,4},{6,7},{7,6},{8,9},{9,8},{10,11... | collective-permute-start | bytes 2064392 | tf_op jit(solution)/shard_map/ppermute | solution.py:32
  35.8 16.5 %copy-start.1 = (bf16[1,1,3584,512]{3,2,1,0:T(8,128)(2,1)S(1)}, bf16[1,1,3584,512]{3,2,1,0:T(8,128)(2,1)}, u32[]{:S(2)}) copy-start(bf16[1,1,3584,512]{3,2,1,0:T(8,128)(2,1)} %param.18) | copy-start | bytes 11010052
  35.8 12.3 %collective-permute-start.8 = (bf16[96,1792]{1,0:T(8,128)(2,1)S(1)}, bf16[96,1792]{1,0:T(8,128)(2,1)S(1)}, u32[]{:S(2)}, u32[]{:S(2)}) collective-permute-start(bf16[96,1792]{1,0:T(8,128)(2,1)S(1)} %get-tuple-element.42), channel_id=1, source_target_pairs={{0,4},{1,3},{2,6},{3,1},{4,0},{5,7},{6,2},{7,5},{8,12},{9,11},{10,... | collective-permute-start | bytes 1032200 | tf_op jit(solution)/shard_map/ppermute | solution.py:27
  38.4 9.8 %collective-permute-start.9 = (bf16[96,1792]{1,0:T(8,128)(2,1)S(1)}, bf16[96,1792]{1,0:T(8,128)(2,1)S(1)}, u32[]{:S(2)}, u32[]{:S(2)}) collective-permute-start(bf16[96,1792]{1,0:T(8,128)(2,1)S(1)} %get-tuple-element.41), channel_id=1, source_target_pairs={{0,1},{1,0},{2,3},{3,2},{4,5},{5,4},{6,7},{7,6},{8,9},{9,8},{10,11... | collective-permute-start | bytes 1032200 | tf_op jit(solution)/shard_map/ppermute | solution.py:32
  38.8 13.0 %collective-permute-start.3 = (bf16[96,1792]{1,0:T(8,128)(2,1)S(1)}, bf16[96,1792]{1,0:T(8,128)(2,1)S(1)}, u32[]{:S(2)}, u32[]{:S(2)}) collective-permute-start(bf16[96,1792]{1,0:T(8,128)(2,1)S(1)} %get-tuple-element.40), channel_id=1, source_target_pairs={{0,4},{1,3},{2,6},{3,1},{4,0},{5,7},{6,2},{7,5},{8,12},{9,11},{10,... | collective-permute-start | bytes 1032200 | tf_op jit(solution)/shard_map/ppermute | solution.py:27
  48.1 3.7 %collective-permute-start.10 = (bf16[96,1792]{1,0:T(8,128)(2,1)S(1)}, bf16[96,1792]{1,0:T(8,128)(2,1)S(1)}, u32[]{:S(2)}, u32[]{:S(2)}) collective-permute-start(bf16[96,1792]{1,0:T(8,128)(2,1)S(1)} %collective-permute-done.8), channel_id=1, source_target_pairs={{0,1},{1,0},{2,3},{3,2},{4,5},{5,4},{6,7},{7,6},{8,9},{9,8},{10,11... | collective-permute-start | bytes 1032200 | tf_op jit(solution)/shard_map/ppermute | solution.py:32
  48.2 7.3 %collective-permute-start.24 = (bf16[96,1792]{1,0:T(8,128)(2,1)S(1)}, bf16[96,1792]{1,0:T(8,128)(2,1)S(1)}, u32[]{:S(2)}, u32[]{:S(2)}) collective-permute-start(bf16[96,1792]{1,0:T(8,128)(2,1)S(1)} %get-tuple-element.34), channel_id=1, source_target_pairs={{0,4},{1,3},{2,6},{3,1},{4,0},{5,7},{6,2},{7,5},{8,12},{9,11},{10,... | collective-permute-start | bytes 1032200 | tf_op jit(solution)/shard_map/ppermute | solution.py:27
  51.8 3.7 %collective-permute-start.4 = (bf16[96,1792]{1,0:T(8,128)(2,1)S(1)}, bf16[96,1792]{1,0:T(8,128)(2,1)S(1)}, u32[]{:S(2)}, u32[]{:S(2)}) collective-permute-start(bf16[96,1792]{1,0:T(8,128)(2,1)S(1)} %get-tuple-element.39), channel_id=1, source_target_pairs={{0,1},{1,0},{2,3},{3,2},{4,5},{5,4},{6,7},{7,6},{8,9},{9,8},{10,11... | collective-permute-start | bytes 1032200 | tf_op jit(solution)/shard_map/ppermute | solution.py:32
  51.8 5.3 %collective-permute-start.5 = (bf16[96,1792]{1,0:T(8,128)(2,1)S(1)}, bf16[96,1792]{1,0:T(8,128)(2,1)S(1)}, u32[]{:S(2)}, u32[]{:S(2)}) collective-permute-start(bf16[96,1792]{1,0:T(8,128)(2,1)S(1)} %collective-permute-done.3), channel_id=1, source_target_pairs={{0,1},{1,0},{2,3},{3,2},{4,5},{5,4},{6,7},{7,6},{8,9},{9,8},{10,11... | collective-permute-start | bytes 1032200 | tf_op jit(solution)/shard_map/ppermute | solution.py:32
  55.5 4.3 %collective-permute-start.25 = (bf16[96,1792]{1,0:T(8,128)(2,1)S(1)}, bf16[96,1792]{1,0:T(8,128)(2,1)S(1)}, u32[]{:S(2)}, u32[]{:S(2)}) collective-permute-start(bf16[96,1792]{1,0:T(8,128)(2,1)S(1)} %get-tuple-element.33), channel_id=1, source_target_pairs={{0,1},{1,0},{2,3},{3,2},{4,5},{5,4},{6,7},{7,6},{8,9},{9,8},{10,11... | collective-permute-start | bytes 1032200 | tf_op jit(solution)/shard_map/ppermute | solution.py:32
  55.5 2.5 %copy-start = (bf16[1,1,3584,512]{3,2,1,0:T(8,128)(2,1)S(1)}, bf16[1,1,3584,512]{3,2,1,0:T(8,128)(2,1)}, u32[]{:S(2)}) copy-start(bf16[1,1,3584,512]{3,2,1,0:T(8,128)(2,1)} %param.17) | copy-start | bytes 11010052
  55.5 7.3 %collective-permute-start.19 = (bf16[96,1792]{1,0:T(8,128)(2,1)S(1)}, bf16[96,1792]{1,0:T(8,128)(2,1)S(1)}, u32[]{:S(2)}, u32[]{:S(2)}) collective-permute-start(bf16[96,1792]{1,0:T(8,128)(2,1)S(1)} %get-tuple-element.32), channel_id=1, source_target_pairs={{0,4},{1,3},{2,6},{3,1},{4,0},{5,7},{6,2},{7,5},{8,12},{9,11},{10,... | collective-permute-start | bytes 1032200 | tf_op jit(solution)/shard_map/ppermute | solution.py:27
  57.1 6.2 %collective-permute-start.26 = (bf16[96,1792]{1,0:T(8,128)(2,1)S(1)}, bf16[96,1792]{1,0:T(8,128)(2,1)S(1)}, u32[]{:S(2)}, u32[]{:S(2)}) collective-permute-start(bf16[96,1792]{1,0:T(8,128)(2,1)S(1)} %collective-permute-done.24), channel_id=1, source_target_pairs={{0,1},{1,0},{2,3},{3,2},{4,5},{5,4},{6,7},{7,6},{8,9},{9,8},{10,11... | collective-permute-start | bytes 1032200 | tf_op jit(solution)/shard_map/ppermute | solution.py:32
  58.8 4.5 %copy-start.2 = (bf16[1,1,512,3584]{3,2,1,0:T(8,128)(2,1)S(1)}, bf16[1,1,512,3584]{3,2,1,0:T(8,128)(2,1)}, u32[]{:S(2)}) copy-start(bf16[1,1,512,3584]{3,2,1,0:T(8,128)(2,1)} %param.19) | copy-start | bytes 11010052
  59.7 4.5 %collective-permute-start.20 = (bf16[96,1792]{1,0:T(8,128)(2,1)S(1)}, bf16[96,1792]{1,0:T(8,128)(2,1)S(1)}, u32[]{:S(2)}, u32[]{:S(2)}) collective-permute-start(bf16[96,1792]{1,0:T(8,128)(2,1)S(1)} %get-tuple-element.31), channel_id=1, source_target_pairs={{0,1},{1,0},{2,3},{3,2},{4,5},{5,4},{6,7},{7,6},{8,9},{9,8},{10,11... | collective-permute-start | bytes 1032200 | tf_op jit(solution)/shard_map/ppermute | solution.py:32
  62.8 1.7 %collective-permute-start.21 = (bf16[96,1792]{1,0:T(8,128)(2,1)S(1)}, bf16[96,1792]{1,0:T(8,128)(2,1)S(1)}, u32[]{:S(2)}, u32[]{:S(2)}) collective-permute-start(bf16[96,1792]{1,0:T(8,128)(2,1)S(1)} %collective-permute-done.19), channel_id=1, source_target_pairs={{0,1},{1,0},{2,3},{3,2},{4,5},{5,4},{6,7},{7,6},{8,9},{9,8},{10,11... | collective-permute-start | bytes 1032200 | tf_op jit(solution)/shard_map/ppermute | solution.py:32
  62.8 5.3 %collective-permute-start.30 = (bf16[96,3584]{1,0:T(8,128)(2,1)S(1)}, bf16[96,3584]{1,0:T(8,128)(2,1)S(1)}, u32[]{:S(2)}, u32[]{:S(2)}) collective-permute-start(bf16[96,3584]{1,0:T(8,128)(2,1)S(1)} %collective-permute-done.28), channel_id=1, source_target_pairs={{0,1},{1,0},{2,3},{3,2},{4,5},{5,4},{6,7},{7,6},{8,9},{9,8},{10,11... | collective-permute-start | bytes 2064392 | tf_op jit(solution)/shard_map/ppermute | solution.py:32
  66.5 7.4 %collective-permute-start.11 = (bf16[192,1792]{1,0:T(8,128)(2,1)S(1)}, bf16[192,1792]{1,0:T(8,128)(2,1)S(1)}, u32[]{:S(2)}, u32[]{:S(2)}) collective-permute-start(bf16[192,1792]{1,0:T(8,128)(2,1)S(1)} %slice.222), channel_id=1, source_target_pairs={{0,1},{1,0},{2,3},{3,2},{4,5},{5,4},{6,7},{7,6},{8,9},{9,8},{10,11... | collective-permute-start | bytes 2064392 | tf_op jit(solution)/shard_map/ppermute | solution.py:32
  67.7 8.0 %collective-permute-start.14 = (bf16[192,1792]{1,0:T(8,128)(2,1)S(1)}, bf16[192,1792]{1,0:T(8,128)(2,1)S(1)}, u32[]{:S(2)}, u32[]{:S(2)}) collective-permute-start(bf16[192,1792]{1,0:T(8,128)(2,1)S(1)} %slice.229), channel_id=1, source_target_pairs={{0,1},{1,0},{2,3},{3,2},{4,5},{5,4},{6,7},{7,6},{8,9},{9,8},{10,11... | collective-permute-start | bytes 2064392 | tf_op jit(solution)/shard_map/ppermute | solution.py:32
  73.7 19.1 %collective-permute-start.31 = (bf16[192,1792]{1,0:T(8,128)(2,1)S(1)}, bf16[192,1792]{1,0:T(8,128)(2,1)S(1)}, u32[]{:S(2)}, u32[]{:S(2)}) collective-permute-start(bf16[192,1792]{1,0:T(8,128)(2,1)S(1)} %slice.241), channel_id=1, source_target_pairs={{0,1},{1,0},{2,3},{3,2},{4,5},{5,4},{6,7},{7,6},{8,9},{9,8},{10,11... | collective-permute-start | bytes 2064392 | tf_op jit(solution)/shard_map/ppermute | solution.py:32
  74.2 7.3 %collective-permute-start.12 = (bf16[96,1792]{1,0:T(8,128)(2,1)S(1)}, bf16[96,1792]{1,0:T(8,128)(2,1)S(1)}, u32[]{:S(2)}, u32[]{:S(2)}) collective-permute-start(bf16[96,1792]{1,0:T(8,128)(2,1)S(1)} %get-tuple-element.36), channel_id=1, source_target_pairs={{0,4},{1,3},{2,6},{3,1},{4,0},{5,7},{6,2},{7,5},{8,12},{9,11},{10,... | collective-permute-start | bytes 1032200 | tf_op jit(solution)/shard_map/ppermute | solution.py:27
  76.1 10.2 %collective-permute-start.15 = (bf16[96,1792]{1,0:T(8,128)(2,1)S(1)}, bf16[96,1792]{1,0:T(8,128)(2,1)S(1)}, u32[]{:S(2)}, u32[]{:S(2)}) collective-permute-start(bf16[96,1792]{1,0:T(8,128)(2,1)S(1)} %get-tuple-element.38), channel_id=1, source_target_pairs={{0,4},{1,3},{2,6},{3,1},{4,0},{5,7},{6,2},{7,5},{8,12},{9,11},{10,... | collective-permute-start | bytes 1032200 | tf_op jit(solution)/shard_map/ppermute | solution.py:27
  81.8 6.1 %collective-permute-start.13 = (bf16[64,1792]{1,0:T(8,128)(2,1)S(1)}, bf16[64,1792]{1,0:T(8,128)(2,1)S(1)}, u32[]{:S(2)}, u32[]{:S(2)}) collective-permute-start(bf16[64,1792]{1,0:T(8,128)(2,1)S(1)} %slice.226), channel_id=1, source_target_pairs={{0,2},{1,5},{2,0},{3,7},{4,6},{5,1},{6,4},{7,3},{8,10},{9,13},{10,... | collective-permute-start | bytes 688136 | tf_op jit(solution)/shard_map/ppermute | solution.py:27
  83.7 10.9 %collective-permute-start.34 = (bf16[192,1792]{1,0:T(8,128)(2,1)S(1)}, bf16[192,1792]{1,0:T(8,128)(2,1)S(1)}, u32[]{:S(2)}, u32[]{:S(2)}) collective-permute-start(bf16[192,1792]{1,0:T(8,128)(2,1)S(1)} %slice.247), channel_id=1, source_target_pairs={{0,1},{1,0},{2,3},{3,2},{4,5},{5,4},{6,7},{7,6},{8,9},{9,8},{10,11... | collective-permute-start | bytes 2064392 | tf_op jit(solution)/shard_map/ppermute | solution.py:32
  86.7 6.1 %collective-permute-start.16 = (bf16[64,1792]{1,0:T(8,128)(2,1)S(1)}, bf16[64,1792]{1,0:T(8,128)(2,1)S(1)}, u32[]{:S(2)}, u32[]{:S(2)}) collective-permute-start(bf16[64,1792]{1,0:T(8,128)(2,1)S(1)} %slice.233), channel_id=1, source_target_pairs={{0,2},{1,5},{2,0},{3,7},{4,6},{5,1},{6,4},{7,3},{8,10},{9,13},{10,... | collective-permute-start | bytes 688136 | tf_op jit(solution)/shard_map/ppermute | solution.py:27
  93.0 8.2 %collective-permute-start.32 = (bf16[96,1792]{1,0:T(8,128)(2,1)S(1)}, bf16[96,1792]{1,0:T(8,128)(2,1)S(1)}, u32[]{:S(2)}, u32[]{:S(2)}) collective-permute-start(bf16[96,1792]{1,0:T(8,128)(2,1)S(1)} %get-tuple-element.28), channel_id=1, source_target_pairs={{0,4},{1,3},{2,6},{3,1},{4,0},{5,7},{6,2},{7,5},{8,12},{9,11},{10,... | collective-permute-start | bytes 1032200 | tf_op jit(solution)/shard_map/ppermute | solution.py:27
  94.9 13.8 %collective-permute-start.35 = (bf16[96,1792]{1,0:T(8,128)(2,1)S(1)}, bf16[96,1792]{1,0:T(8,128)(2,1)S(1)}, u32[]{:S(2)}, u32[]{:S(2)}) collective-permute-start(bf16[96,1792]{1,0:T(8,128)(2,1)S(1)} %get-tuple-element.30), channel_id=1, source_target_pairs={{0,4},{1,3},{2,6},{3,1},{4,0},{5,7},{6,2},{7,5},{8,12},{9,11},{10,... | collective-permute-start | bytes 1032200 | tf_op jit(solution)/shard_map/ppermute | solution.py:27
  101.6 8.1 %collective-permute-start.33 = (bf16[64,1792]{1,0:T(8,128)(2,1)S(1)}, bf16[64,1792]{1,0:T(8,128)(2,1)S(1)}, u32[]{:S(2)}, u32[]{:S(2)}) collective-permute-start(bf16[64,1792]{1,0:T(8,128)(2,1)S(1)} %slice.245), channel_id=1, source_target_pairs={{0,2},{1,5},{2,0},{3,7},{4,6},{5,1},{6,4},{7,3},{8,10},{9,13},{10,... | collective-permute-start | bytes 688136 | tf_op jit(solution)/shard_map/ppermute | solution.py:27
  109.0 6.1 %collective-permute-start.36 = (bf16[64,1792]{1,0:T(8,128)(2,1)S(1)}, bf16[64,1792]{1,0:T(8,128)(2,1)S(1)}, u32[]{:S(2)}, u32[]{:S(2)}) collective-permute-start(bf16[64,1792]{1,0:T(8,128)(2,1)S(1)} %slice.251), channel_id=1, source_target_pairs={{0,2},{1,5},{2,0},{3,7},{4,6},{5,1},{6,4},{7,3},{8,10},{9,13},{10,... | collective-permute-start | bytes 688136 | tf_op jit(solution)/shard_map/ppermute | solution.py:27
